TPU v7x, 512 devices: a 8x2x16 block of a 8x8x16 slice. The times are simulated.
512 devices in a mesh: parts: 2 (over y), tile: 128 (over x, z), cond: 2 (over core).
Axes of the slice: x: 8, y: 2, z: 16, core: 2. Of those that a mesh axis runs over, the one named last changes fastest.
The devices are a block of a 8x8x16 slice.
Arguments:
- mask: bfloat16 [256, 256, 256], P(('parts', 'tile')), parts along dimension 0, may hold values from -1 to 1
- kernels: bfloat16 [8, 24, 64, 128], P('cond'), may hold values from -6 to 6
- socs_weight: float32 [8, 24], P('cond'), may hold values from 0.02 to 1
- dose: float32 [8], P('cond'), may hold values from 0.8 to 1.25
- threshold: float32 [8], P('cond'), may hold values from 0.5 to 0.85
Outputs:
- band_max: float32 [256, 256, 256], P(('parts', 'tile'), 'cond'), parts along dimension 0
- band_min: float32 [256, 256, 256], P(('parts', 'tile'), 'cond'), parts along dimension 0
There are 2 independent parts, one for each index of `parts`. A program takes and returns all parts, laid end to end along the dimension named above; an argument that names none is the same for every part. Nothing has to cross between parts.
All inputs are finite; a program needn't handle non-finite values.
Results may differ from a plain program's by a relative error of at most 0.0068.
Values may be sent and summed in bfloat16 or wider, within the bound.
A program may use at most 64 MiB of HBM per device.

v0:
```python
import math

import jax
import jax.numpy as jnp
from jax import lax
from jax.sharding import PartitionSpec as P

MARGIN = 64
BLUR = 8


diffusion = 2.0
steepness = 8.0


def shifted(block, axis, distance):
    devices = range(lax.axis_size(axis))
    route = [((i - distance) % len(devices), i) for i in devices]
    return lax.ppermute(block, axis, route)


def in_one_piece(arrays, axis, split_dim, concat_dim, along):
    both = jnp.concatenate(arrays, axis=along)
    filled, at, outs = (
        lax.all_to_all(both, axis, split_axis=split_dim, concat_axis=concat_dim, tiled=True),
        0,
        [],
    )
    for a in arrays:
        outs.append(lax.slice_in_dim(filled, at, at + a.shape[along], axis=along))
        at += a.shape[along]
    return tuple(outs)


def phase_table(first, count, pad_width, band_width):
    pixel_index = jnp.arange(count, dtype=jnp.int32) + first
    freq_index = (jnp.arange(band_width, dtype=jnp.int32) - band_width // 2) % pad_width
    turn_count = pixel_index[:, None] * freq_index[None, :] % pad_width
    angle_grid = turn_count.astype(jnp.float32) * (2.0 * math.pi / pad_width)
    return (jnp.cos(angle_grid).astype(jnp.bfloat16), jnp.sin(angle_grid).astype(jnp.bfloat16))


def blur_table(core):
    offset_grid = (
        jnp.arange(core + 2 * BLUR, dtype=jnp.int32)[None, :]
        - jnp.arange(core, dtype=jnp.int32)[:, None]
        - BLUR
    )
    distance = offset_grid.astype(jnp.float32)
    taps_grid = jnp.exp(-distance * distance / (2.0 * diffusion * diffusion))
    taps_grid = jnp.where(jnp.abs(offset_grid) <= BLUR, taps_grid, jnp.zeros_like(taps_grid))
    reach_grid = jnp.arange(-BLUR, BLUR + 1, dtype=jnp.int32).astype(jnp.float32)
    total_taps = jnp.sum(jnp.exp(-reach_grid * reach_grid / (2.0 * diffusion * diffusion)))
    return taps_grid / total_taps


def make_tables(core, band_width):
    pad_width = core + 2 * MARGIN
    cos_in, sin_in = phase_table(0, pad_width, pad_width, band_width)
    cos_out, sin_out = phase_table(MARGIN - BLUR, core + 2 * BLUR, pad_width, band_width)
    return (cos_in, sin_in, cos_out, sin_out, blur_table(core))


def expose(window, kernel_set, weights, dose_one, threshold_one, tables):
    cos_in, sin_in, cos_out, sin_out, blur_rows = tables
    pad_width = window.shape[0]
    band_width = cos_in.shape[1]
    part_real = jnp.dot(cos_in.T, window, preferred_element_type=jnp.float32).astype(jnp.bfloat16)
    part_imag = (-jnp.dot(sin_in.T, window, preferred_element_type=jnp.float32)).astype(
        jnp.bfloat16
    )
    spec_real = (
        jnp.dot(part_real, cos_in, preferred_element_type=jnp.float32)
        + jnp.dot(part_imag, sin_in, preferred_element_type=jnp.float32)
    ) / pad_width
    spec_imag = (
        jnp.dot(part_imag, cos_in, preferred_element_type=jnp.float32)
        - jnp.dot(part_real, sin_in, preferred_element_type=jnp.float32)
    ) / pad_width
    group_size = min(8, kernel_set.shape[0])
    kernel_groups = kernel_set.reshape(-1, group_size, band_width, 2 * band_width)
    weight_groups = weights.reshape(-1, group_size)

    def group_power(packed):
        kernel_part, weight_part = packed
        kern_real = kernel_part[:, :, :band_width].astype(jnp.float32)
        kern_imag = kernel_part[:, :, band_width:].astype(jnp.float32)
        prod_real = (spec_real * kern_real - spec_imag * kern_imag).astype(jnp.bfloat16)
        prod_imag = (spec_real * kern_imag + spec_imag * kern_real).astype(jnp.bfloat16)
        half_real = (
            jnp.einsum("nfg,yg->nfy", prod_real, cos_out, preferred_element_type=jnp.float32)
            - jnp.einsum("nfg,yg->nfy", prod_imag, sin_out, preferred_element_type=jnp.float32)
        ).astype(jnp.bfloat16)
        half_imag = (
            jnp.einsum("nfg,yg->nfy", prod_real, sin_out, preferred_element_type=jnp.float32)
            + jnp.einsum("nfg,yg->nfy", prod_imag, cos_out, preferred_element_type=jnp.float32)
        ).astype(jnp.bfloat16)
        field_real = (
            jnp.einsum("xf,nfy->nxy", cos_out, half_real, preferred_element_type=jnp.float32)
            - jnp.einsum("xf,nfy->nxy", sin_out, half_imag, preferred_element_type=jnp.float32)
        ) / band_width
        field_imag = (
            jnp.einsum("xf,nfy->nxy", cos_out, half_imag, preferred_element_type=jnp.float32)
            + jnp.einsum("xf,nfy->nxy", sin_out, half_real, preferred_element_type=jnp.float32)
        ) / band_width
        power = field_real * field_real + field_imag * field_imag
        return jnp.tensordot(weight_part, power, axes=1)

    intensity = jnp.sum(lax.map(group_power, (kernel_groups, weight_groups)), axis=0) / jnp.sum(
        weights
    )
    blurred = jnp.dot(jnp.dot(blur_rows, intensity), blur_rows.T)
    return jax.nn.sigmoid(steepness * (dose_one * blurred - threshold_one))


def from_rows(piece, offset):
    return shifted(piece, "tile", offset)


def from_cols(piece, offset):
    return shifted(piece, "tile", offset)


def masked_by(flag, piece):
    return jnp.where(flag, piece, jnp.zeros_like(piece))


def gather_margins(tile_mask):
    count = lax.axis_size("tile")
    columns = min(8, count // 2)
    grid_rows = count // columns
    position = (lax.axis_index("tile") + columns // 2) % count
    column = position % columns
    row = position // columns
    has_left = column > 0
    has_right = column < columns - 1
    has_up = row > 0
    has_down = row < grid_rows - 1
    margin_rows = MARGIN
    upper_rows = masked_by(has_up, from_rows(tile_mask[-margin_rows:], columns))
    lower_rows = masked_by(has_down, from_rows(tile_mask[:margin_rows], -columns))
    tall_block = jnp.concatenate([upper_rows, tile_mask, lower_rows], axis=0)
    left_part = masked_by(has_left, from_cols(tall_block[:, -margin_rows:], 1))
    right_part = masked_by(has_right, from_cols(tall_block[:, :margin_rows], -1))
    return jnp.concatenate([left_part, tall_block, right_part], axis=1)


def on_device(mask, kernels, socs_weight, dose, threshold):
    core = mask.shape[1]
    window = gather_margins(mask[0])
    tables = make_tables(core, kernels.shape[2])

    def one_condition(packed):
        kernel_set, weights, dose_one, threshold_one = packed
        return expose(window, kernel_set, weights, dose_one, threshold_one, tables)

    resist = lax.map(one_condition, (kernels, socs_weight, dose, threshold))
    highest = jnp.max(resist, axis=0)
    lowest = jnp.min(resist, axis=0)
    pieces_high, pieces_low = in_one_piece((highest[None], lowest[None]), "cond", 1, 0, 2)
    top_band = jnp.max(pieces_high, axis=0)
    bottom_band = jnp.min(pieces_low, axis=0)
    return (top_band[None], bottom_band[None])


def solution(mesh):
    return jax.shard_map(
        on_device,
        mesh=mesh,
        in_specs=(
            P(("parts", "tile"), None, None),
            P("cond", None, None, None),
            P("cond", None),
            P("cond"),
            P("cond"),
        ),
        out_specs=(P(("parts", "tile"), "cond", None), P(("parts", "tile"), "cond", None)),
        check_vma=False,
    )
```

profile of v0, /device:TPU:65, one launch (start us, length us, event | category | flops | bytes accessed | tf_op | source)
XLA Modules:
  0.0 238.2 jit_solution(7327325409062985319)
XLA Ops:
  1.4 33.7 %collective-permute-start = (bf16[64,256]{1,0:T(8,128)(2,1)S(1)}, bf16[64,256]{1,0:T(8,128)(2,1)S(1)}, u32[]{:S(2)}, u32[]{:S(2)}) collective-permute-start(bf16[64,256]{1,0:T(8,128)(2,1)S(1)} %get-tuple-element.405), channel_id=1, source_target_pairs={{240,0},{242,2},{244,4},{246,6},{248,8},{250,10},{252,12},{254,14}... | collective-permute-start | bytes 98312 | tf_op jit(solution)/shard_map/ppermute | solution.py:19
  35.1 5.2 %collective-permute-start.1 = (bf16[64,256]{1,0:T(8,128)(2,1)S(1)}, bf16[64,256]{1,0:T(8,128)(2,1)S(1)}, u32[]{:S(2)}, u32[]{:S(2)}) collective-permute-start(bf16[64,256]{1,0:T(8,128)(2,1)S(1)} %get-tuple-element.406), channel_id=1, source_target_pairs={{16,0},{18,2},{20,4},{22,6},{24,8},{26,10},{28,12},{30,14},{32,16}... | collective-permute-start | bytes 98312 | tf_op jit(solution)/shard_map/ppermute | solution.py:19
  40.4 8.1 %collective-permute-done.1 = bf16[64,256]{1,0:T(8,128)(2,1)S(1)} collective-permute-done((bf16[64,256]{1,0:T(8,128)(2,1)S(1)}, bf16[64,256]{1,0:T(8,128)(2,1)S(1)}, u32[]{:S(2)}, u32[]{:S(2)}) %collective-permute-start.1) | collective-permute-done | bytes 32800 | tf_op jit(solution)/shard_map/ppermute | solution.py:19
  49.5 5.0 %collective-permute-start.2 = (bf16[384,64]{1,0:T(8,128)(2,1)S(1)}, bf16[384,64]{1,0:T(8,128)(2,1)S(1)}, u32[]{:S(2)}, u32[]{:S(2)}) collective-permute-start(bf16[384,64]{1,0:T(8,128)(2,1)S(1)} %get-tuple-element.403), channel_id=1, source_target_pairs={{254,0},{0,2},{2,4},{4,6},{6,8},{8,10},{10,12},{12,14},{14,16},{16... | collective-permute-start | bytes 147464 | tf_op jit(solution)/shard_map/ppermute | solution.py:19
  55.3 15.1 %collective-permute-start.3 = (bf16[384,64]{1,0:T(8,128)(2,1)S(1)}, bf16[384,64]{1,0:T(8,128)(2,1)S(1)}, u32[]{:S(2)}, u32[]{:S(2)}) collective-permute-start(bf16[384,64]{1,0:T(8,128)(2,1)S(1)} %get-tuple-element.404), channel_id=1, source_target_pairs={{2,0},{4,2},{6,4},{8,6},{10,8},{12,10},{14,12},{16,14},{18,16},{20... | collective-permute-start | bytes 147464 | tf_op jit(solution)/shard_map/ppermute | solution.py:19
  70.5 1.6 collective-permute-done.3
  72.1 1.1 pad_maximum_fusion.1
  77.8 1.5 convolution_add_fusion.1
  79.3 149.4 %while.36 = (s32[]{:T(128)}, f32[4,256,256]{2,1,0:T(8,128)}, f32[4]{0:T(128)S(1)}, bf16[4,24,64,128]{3,2,1,0:T(8,128)(2,1)}, f32[4,24]{1,0:T(4,128)}, /*index=5*...) while((s32[]{:T(128)}, f32[4,256,256]{2,1,0:T(8,128)}, ...), condition=%wide.region_6.7_spmd.clone.clone.clone, body=%wide.region_1.6_spmd.clone.clone.clone.sunk | while | flops 457342752 | bytes 29373336 | solution.py:157
  79.3 1.4 fusion.185
  80.7 1.8 constant_dynamic-slice_fusion.4
  83.8 25.7 %while.37 = (s32[]{:T(128)}, f32[3,272,272]{2,1,0:T(8,128)}, bf16[3,8]{1,0:T(4,128)(2,1)S(1)}, f32[64,64]{1,0:T(8,128)S(1)}, bf16[3,8,64,128]{3,2,1,0:T(8,128)(2...) while((s32[]{:T(128)}, f32[3,272,272]{2,1,0:T(8,128)}, ...), condition=%wide.region_3.3_spmd.clone, body=%wide.region_2.2_spmd.clone.sunk | while | flops 381603840 | bytes 26704996 | solution.py:109
  88.9 2.0 copy.14
  96.4 1.1 add_bitcast_fusion.2
  97.5 2.0 copy.14
  106.1 2.0 copy.14
  109.5 1.4 reduce_sum.43
  110.9 1.2 dynamic_slice.64
  112.7 3.9 %fusion.186 = f32[4,256,256]{2,1,0:T(8,128)} fusion(f32[4,256,256]{2,1,0:T(8,128)} %get-tuple-element.597, s32[]{:T(128)} %get-tuple-element.596, f32[272,272]{1,0:T(8,128)S(1)} %reduce_sum.43, f32[]{:T(128)} %get-tuple-element.544, f32[]{:T(128)} %get-tuple-element.621, f32[]{:T(128)} %bitcast.76, f32[]{:T(128)} %bitcast.77), kind=kOutput, calls=%fused_computation.44.clone.1 | convolution fusion | flops 75391232 | bytes 561152 | tf_op jit(solution)/shard_map/while/body/eval_jaxpr/dot_general | solution.py:112
  116.6 1.4 fusion.185
  118.1 1.8 constant_dynamic-slice_fusion.4
  121.1 25.7 %while.37 = (s32[]{:T(128)}, f32[3,272,272]{2,1,0:T(8,128)}, bf16[3,8]{1,0:T(4,128)(2,1)S(1)}, f32[64,64]{1,0:T(8,128)S(1)}, bf16[3,8,64,128]{3,2,1,0:T(8,128)(2...) while((s32[]{:T(128)}, f32[3,272,272]{2,1,0:T(8,128)}, ...), condition=%wide.region_3.3_spmd.clone, body=%wide.region_2.2_spmd.clone.sunk | while | flops 381603840 | bytes 26704996 | solution.py:109
  126.3 2.0 copy.14
  134.8 2.0 copy.14
  143.4 2.0 copy.14
  146.8 1.4 reduce_sum.43
  148.3 1.2 dynamic_slice.64
  150.1 3.9 %fusion.186 = f32[4,256,256]{2,1,0:T(8,128)} fusion(f32[4,256,256]{2,1,0:T(8,128)} %get-tuple-element.597, s32[]{:T(128)} %get-tuple-element.596, f32[272,272]{1,0:T(8,128)S(1)} %reduce_sum.43, f32[]{:T(128)} %get-tuple-element.544, f32[]{:T(128)} %get-tuple-element.621, f32[]{:T(128)} %bitcast.76, f32[]{:T(128)} %bitcast.77), kind=kOutput, calls=%fused_computation.44.clone.1 | convolution fusion | flops 75391232 | bytes 561152 | tf_op jit(solution)/shard_map/while/body/eval_jaxpr/dot_general | solution.py:112
  154.0 1.4 fusion.185
  155.4 1.8 constant_dynamic-slice_fusion.4
  158.4 25.7 %while.37 = (s32[]{:T(128)}, f32[3,272,272]{2,1,0:T(8,128)}, bf16[3,8]{1,0:T(4,128)(2,1)S(1)}, f32[64,64]{1,0:T(8,128)S(1)}, bf16[3,8,64,128]{3,2,1,0:T(8,128)(2...) while((s32[]{:T(128)}, f32[3,272,272]{2,1,0:T(8,128)}, ...), condition=%wide.region_3.3_spmd.clone, body=%wide.region_2.2_spmd.clone.sunk | while | flops 381603840 | bytes 26704996 | solution.py:109
  163.6 2.0 copy.14
  172.1 2.0 copy.14
  180.7 2.0 copy.14
  184.2 1.4 reduce_sum.43
  185.6 1.2 dynamic_slice.64
  187.4 3.9 %fusion.186 = f32[4,256,256]{2,1,0:T(8,128)} fusion(f32[4,256,256]{2,1,0:T(8,128)} %get-tuple-element.597, s32[]{:T(128)} %get-tuple-element.596, f32[272,272]{1,0:T(8,128)S(1)} %reduce_sum.43, f32[]{:T(128)} %get-tuple-element.544, f32[]{:T(128)} %get-tuple-element.621, f32[]{:T(128)} %bitcast.76, f32[]{:T(128)} %bitcast.77), kind=kOutput, calls=%fused_computation.44.clone.1 | convolution fusion | flops 75391232 | bytes 561152 | tf_op jit(solution)/shard_map/while/body/eval_jaxpr/dot_general | solution.py:112
  191.3 1.4 fusion.185
  192.8 1.8 constant_dynamic-slice_fusion.4
  195.8 25.8 %while.37 = (s32[]{:T(128)}, f32[3,272,272]{2,1,0:T(8,128)}, bf16[3,8]{1,0:T(4,128)(2,1)S(1)}, f32[64,64]{1,0:T(8,128)S(1)}, bf16[3,8,64,128]{3,2,1,0:T(8,128)(2...) while((s32[]{:T(128)}, f32[3,272,272]{2,1,0:T(8,128)}, ...), condition=%wide.region_3.3_spmd.clone, body=%wide.region_2.2_spmd.clone.sunk | while | flops 381603840 | bytes 26704996 | solution.py:109
  201.0 2.0 copy.14
  209.5 2.0 copy.14
  218.1 2.0 copy.14
  221.5 1.4 reduce_sum.43
  223.0 1.2 dynamic_slice.64
  224.8 3.9 %fusion.186 = f32[4,256,256]{2,1,0:T(8,128)} fusion(f32[4,256,256]{2,1,0:T(8,128)} %get-tuple-element.597, s32[]{:T(128)} %get-tuple-element.596, f32[272,272]{1,0:T(8,128)S(1)} %reduce_sum.43, f32[]{:T(128)} %get-tuple-element.544, f32[]{:T(128)} %get-tuple-element.621, f32[]{:T(128)} %bitcast.76, f32[]{:T(128)} %bitcast.77), kind=kOutput, calls=%fused_computation.44.clone.1 | convolution fusion | flops 75391232 | bytes 561152 | tf_op jit(solution)/shard_map/while/body/eval_jaxpr/dot_general | solution.py:112
  228.7 1.4 fusion.136
  231.0 6.4 %all_to_all.12 = f32[1,256,512]{2,0,1:T(1,128)S(1)} all-to-all(f32[1,256,512]{2,0,1:T(1,128)S(1)} %pad_maximum_fusion), channel_id=1, replica_groups=mesh['parts'=2,'tile'=128,'cond'=2] {'cond'}, dimensions={1} | all-to-all | bytes 1048576 | tf_op jit(solution)/shard_map/all_to_all | solution.py:25
  (176 shorter events, 93.1 us)
Async XLA Ops:
  0.6 78.7 %copy-start = (f32[4]{0:T(128)S(1)}, f32[4]{0:T(128)}, u32[]{:S(2)}) copy-start(f32[4]{0:T(128)} %param.12) | copy-start | bytes 52
  1.4 38.9 %collective-permute-start = (bf16[64,256]{1,0:T(8,128)(2,1)S(1)}, bf16[64,256]{1,0:T(8,128)(2,1)S(1)}, u32[]{:S(2)}, u32[]{:S(2)}) collective-permute-start(bf16[64,256]{1,0:T(8,128)(2,1)S(1)} %get-tuple-element.405), channel_id=1, source_target_pairs={{240,0},{242,2},{244,4},{246,6},{248,8},{250,10},{252,12},{254,14}... | collective-permute-start | bytes 98312 | tf_op jit(solution)/shard_map/ppermute | solution.py:19
  35.1 13.4 %collective-permute-start.1 = (bf16[64,256]{1,0:T(8,128)(2,1)S(1)}, bf16[64,256]{1,0:T(8,128)(2,1)S(1)}, u32[]{:S(2)}, u32[]{:S(2)}) collective-permute-start(bf16[64,256]{1,0:T(8,128)(2,1)S(1)} %get-tuple-element.406), channel_id=1, source_target_pairs={{16,0},{18,2},{20,4},{22,6},{24,8},{26,10},{28,12},{30,14},{32,16}... | collective-permute-start | bytes 98312 | tf_op jit(solution)/shard_map/ppermute | solution.py:19
  49.5 20.9 %collective-permute-start.2 = (bf16[384,64]{1,0:T(8,128)(2,1)S(1)}, bf16[384,64]{1,0:T(8,128)(2,1)S(1)}, u32[]{:S(2)}, u32[]{:S(2)}) collective-permute-start(bf16[384,64]{1,0:T(8,128)(2,1)S(1)} %get-tuple-element.403), channel_id=1, source_target_pairs={{254,0},{0,2},{2,4},{4,6},{6,8},{8,10},{10,12},{12,14},{14,16},{16... | collective-permute-start | bytes 147464 | tf_op jit(solution)/shard_map/ppermute | solution.py:19
  55.3 16.7 %collective-permute-start.3 = (bf16[384,64]{1,0:T(8,128)(2,1)S(1)}, bf16[384,64]{1,0:T(8,128)(2,1)S(1)}, u32[]{:S(2)}, u32[]{:S(2)}) collective-permute-start(bf16[384,64]{1,0:T(8,128)(2,1)S(1)} %get-tuple-element.404), channel_id=1, source_target_pairs={{2,0},{4,2},{6,4},{8,6},{10,8},{12,10},{14,12},{16,14},{18,16},{20... | collective-permute-start | bytes 147464 | tf_op jit(solution)/shard_map/ppermute | solution.py:19
where the time goes:
time: 240 us; the launch traced here: 238 us
  matrix products  78.9 us (33%)
  local copies, waits for them, and re-layouts  61 us (25%)
  starting transfers between devices  59 us (25%)
  other arithmetic  21.5 us (9%)
  waiting for transfers between devices  9.7 us (4%)
  blocking collectives  6.44 us (3%)
    ppermute x4, starting transfers between devices, shifted(): return lax.ppermute(block, axis, route)  59 us
    add x12, local copies, waits for them, and re-layouts, group_power(): power = field_real * field_real + field_imag * field_imag  24.6 us
    dot_general x4, matrix products, expose(): blurred = jnp.dot(jnp.dot(blur_rows, intensity), blur_rows.T)  15.6 us
    dynamic_slice x12, local copies, waits for them, and re-layouts, on_device(): resist = lax.map(one_condition, (kernels, socs_weight, dose, threshold))  14.3 us
    dot_general x12, matrix products, group_power(): jnp.einsum('xf,nfy->nxy', sin_out, half_real, preferred_element_type=jnp....  12.8 us
    squeeze x12, local copies, waits for them, and re-layouts, expose(): lax.map(group_power, (kernel_groups, weight_groups))  11 us
    ppermute x4, waiting for transfers between devices, shifted(): return lax.ppermute(block, axis, route)  9.7 us
    dynamic_update_slice x12, local copies, waits for them, and re-layouts, expose(): lax.map(group_power, (kernel_groups, weight_groups))  9.48 us
  transfers between devices with their start and end apart: 4, of which 2 were waited for; matrix products, arithmetic and copies ran while one was open for 0% of the time, Pallas kernels for 0%

commit v1 on v0

v1 whole, which is shorter than its diff:
```python
import functools

import jax
import jax.numpy as jnp
import numpy as np
from jax import lax
from jax.experimental import pallas as pl
from jax.experimental.pallas import tpu as pltpu
from jax.sharding import PartitionSpec as P

MESH = pl.DeviceIdType.MESH
MARGIN = 64
BLUR = 8
LANES = 128
STEP = 3
PACK = 4

diffusion = 2.0
steepness = 8.0


def phase(pixels, pad_width, band_width):
    freq = np.arange(band_width) - band_width // 2
    angle = 2.0 * np.pi * ((pixels[:, None] * freq[None, :]) % pad_width) / pad_width
    return np.cos(angle), np.sin(angle)


def make_tables(core, band_width):
    pad_width = core + 2 * MARGIN
    bf16 = lambda a: np.asarray(a, np.float32).astype(jnp.bfloat16)
    cos_in, sin_in = phase(np.arange(pad_width), pad_width, band_width)
    both = np.concatenate([cos_in, -sin_in], axis=1)
    gap = np.zeros((LANES - MARGIN, 2 * band_width))
    columns = np.concatenate([gap, both, gap], axis=0)
    rows = np.concatenate([cos_in.T, sin_in.T], axis=0)
    own_rows = rows[:, MARGIN : MARGIN + core]
    far_rows = np.concatenate([rows[:, :MARGIN], rows[:, MARGIN + core :]], axis=1)
    count = pad_width // STEP
    cos_s, sin_s = phase(np.arange(count) * STEP, pad_width, band_width)
    first = np.block([[cos_s, -sin_s, -sin_s, cos_s], [sin_s, cos_s, cos_s, sin_s]])
    nil = np.zeros((band_width, count))
    second = np.block(
        [
            [cos_s.T, sin_s.T, nil, nil],
            [nil, nil, cos_s.T, sin_s.T],
            [-sin_s.T, cos_s.T, nil, nil],
            [nil, nil, -sin_s.T, cos_s.T],
        ]
    )
    offset = np.arange(core + 2 * BLUR)[None, :] - np.arange(core)[:, None] - BLUR
    taps = np.where(np.abs(offset) <= BLUR, np.exp(-(offset**2) / (2.0 * diffusion**2)), 0.0)
    reach = np.arange(-BLUR, BLUR + 1)
    taps = taps / np.sum(np.exp(-(reach**2) / (2.0 * diffusion**2)))
    pixel = np.arange(MARGIN - BLUR, MARGIN + core + BLUR)
    wave = np.arange(-(band_width - 1), band_width)
    apart = pixel[:, None] - STEP * np.arange(count)[None, :]
    interpolate = np.cos(2.0 * np.pi * apart[:, :, None] * wave / pad_width).sum(-1) / count
    smooth = np.asarray(taps @ interpolate, np.float32)
    high = bf16(smooth).astype(np.float32)
    low = smooth - high
    rows_out = np.concatenate([high, low, high], axis=1)
    cols_out = np.concatenate([high.T, low.T, high.T], axis=0)
    half = core // 2
    rows_out = rows_out.reshape(2, half, 3 * count)
    return tuple(bf16(a) for a in (columns, own_rows, far_rows, first, second, rows_out, cols_out))


def nt_dot(a, b):
    return lax.dot_general(a, b, (((1,), (1,)), ((), ())), preferred_element_type=jnp.float32)


def dot(a, b):
    return jnp.dot(a, b, preferred_element_type=jnp.float32)


def halves(a):
    high = a.astype(jnp.bfloat16)
    return high, (a - high.astype(jnp.float32)).astype(jnp.bfloat16)


def kernel(
    tiles,
    weight_ref,
    dose_ref,
    threshold_ref,
    mask_hbm,
    kernels_hbm,
    columns_hbm,
    own_rows_hbm,
    far_rows_hbm,
    first_hbm,
    second_hbm,
    rows_out_hbm,
    cols_out_hbm,
    high_ref,
    low_ref,
    mask_v,
    kernels_v,
    columns_v,
    own_rows_v,
    far_rows_v,
    first_v,
    second_v,
    rows_out_v,
    cols_out_v,
    left_v,
    right_v,
    spec_rows,
    far_v,
    own_level,
    sib_level,
    load_sem,
    send_sem,
    recv_sem,
    level_send,
    level_recv,
):
    conds, kerns, band = kernels_v.shape[:3]
    core = mask_v.shape[0]
    tile = lax.axis_index("tile")
    cond = lax.axis_index("cond")
    grid_cols = min(8, tiles // 2)
    grid_rows = tiles // grid_cols
    place = lax.rem(tile + grid_cols // 2, tiles)
    column = lax.rem(place, grid_cols)
    row = lax.div(place, grid_cols)
    right = {"tile": lax.rem(tile + 1, tiles)}
    left = {"tile": lax.rem(tile + tiles - 1, tiles)}
    down = {"tile": lax.rem(tile + grid_cols, tiles)}
    up = {"tile": lax.rem(tile + tiles - grid_cols, tiles)}
    sibling = {"cond": 1 - cond}

    barrier = pltpu.get_barrier_semaphore()
    for peer in (up, down, left, right, sibling):
        pl.semaphore_signal(barrier, inc=1, device_id=peer, device_id_type=MESH)

    sources = (
        mask_hbm.at[0],
        columns_hbm,
        own_rows_hbm,
        far_rows_hbm,
        first_hbm,
        second_hbm,
        rows_out_hbm,
        cols_out_hbm,
    )
    targets = (
        mask_v,
        columns_v,
        own_rows_v,
        far_rows_v,
        first_v,
        second_v,
        rows_out_v,
        cols_out_v,
    )
    loads = [
        pltpu.make_async_copy(s, t, load_sem.at[i]) for i, (s, t) in enumerate(zip(sources, targets))
    ]
    for c in range(conds):
        loads.append(
            pltpu.make_async_copy(kernels_hbm.at[c], kernels_v.at[c], load_sem.at[len(sources) + c])
        )
    for load in loads:
        load.start()
    for load in loads:
        load.wait()

    def remote(src, dst, i, peer):
        return pltpu.make_async_remote_copy(
            src_ref=src,
            dst_ref=dst,
            send_sem=send_sem.at[i],
            recv_sem=recv_sem.at[i],
            device_id=peer,
            device_id_type=MESH,
        )

    to_right = remote(mask_v.at[:, core - LANES :], left_v, 0, right)
    to_left = remote(mask_v.at[:, :LANES], right_v, 1, left)
    to_down = remote(spec_rows.at[core - MARGIN :], far_v.at[:MARGIN], 2, down)
    to_up = remote(spec_rows.at[:MARGIN], far_v.at[MARGIN:], 3, up)

    pl.semaphore_wait(barrier, 5)
    to_right.start()
    to_left.start()

    part = dot(mask_v[...], columns_v[LANES : LANES + core])
    to_right.wait_recv()
    zero = jnp.zeros((core, LANES), jnp.bfloat16)
    part += dot(jnp.where(column > 0, left_v[...], zero), columns_v[:LANES])
    to_left.wait_recv()
    part += dot(
        jnp.where(column < grid_cols - 1, right_v[...], zero), columns_v[LANES + core :]
    )
    spec_rows[...] = part.astype(jnp.bfloat16)
    to_down.start()
    to_up.start()
    mixed = dot(own_rows_v[...], spec_rows[...])
    to_down.wait_recv()
    to_up.wait_recv()
    zero = jnp.zeros((MARGIN, 2 * band), jnp.bfloat16)
    above = jnp.where(row > 0, far_v[:MARGIN], zero)
    below = jnp.where(row < grid_rows - 1, far_v[MARGIN:], zero)
    mixed += dot(far_rows_v[...], jnp.concatenate([above, below], axis=0))
    mixed *= 1.0 / ((core + 2 * MARGIN) * band)
    lower = lax.broadcasted_iota(jnp.int32, (band, 2 * band), 1) < band
    turned = pltpu.roll(mixed[band:], band, axis=1)
    spec = mixed[:band] + jnp.where(lower, turned, -turned)
    swapped = pltpu.roll(spec, band, axis=1)
    reals = jnp.where(lower, spec, swapped)
    imags = jnp.where(lower, swapped, -spec)
    spec_one = jnp.concatenate([reals, imags], axis=1)

    count = own_level.shape[1]
    level_copies = []
    for c in range(conds):

        def group(g, level, c=c):
            held = kernels_v[c, pl.ds(g * PACK, PACK)].astype(jnp.float32)
            rows = []
            for j in range(PACK):
                rows.append(
                    (spec_one * jnp.concatenate([held[j], held[j]], axis=1)).astype(jnp.bfloat16)
                )
            packed = jnp.concatenate(rows, axis=0)
            half = nt_dot(first_v[...], packed).astype(jnp.bfloat16)
            for j in range(PACK // 2):
                span = slice(j * 2 * band, (j + 1) * 2 * band)
                pair = jnp.concatenate([half[:count, span], half[count:, span]], axis=1)
                field = dot(pair, second_v[...])
                for i in range(2):
                    re = field[:, 2 * i * count : (2 * i + 1) * count]
                    im = field[:, (2 * i + 1) * count : (2 * i + 2) * count]
                    level += weight_ref[c, g * PACK + 2 * j + i] * (re * re + im * im)
            return level

        level = lax.fori_loop(
            0, kerns // PACK, group, jnp.zeros((count, count), jnp.float32), unroll=True
        )
        total = weight_ref[c, 0]
        for k in range(1, kerns):
            total += weight_ref[c, k]
        scale = jnp.full((1, count), steepness * dose_ref[c]) / jnp.full((1, count), total)
        own_level[c] = level * scale - steepness * threshold_ref[c]
        copy = pltpu.make_async_remote_copy(
            src_ref=own_level.at[c],
            dst_ref=sib_level.at[c],
            send_sem=level_send.at[c],
            recv_sem=level_recv.at[c],
            device_id=sibling,
            device_id_type=MESH,
        )
        copy.start()
        level_copies.append(copy)

    rows_out = rows_out_v[cond]
    high = low = None
    for i in range(2 * conds):
        if i < conds:
            level = own_level[i]
        else:
            level_copies[i - conds].wait_recv()
            level = sib_level[i - conds]
        fine, rest = halves(level)
        tall = nt_dot(rows_out, jnp.concatenate([fine, fine, rest], axis=1))
        fine, rest = halves(tall)
        logit = dot(jnp.concatenate([fine, fine, rest], axis=1), cols_out_v[...])
        high = logit if high is None else jnp.maximum(high, logit)
        low = logit if low is None else jnp.minimum(low, logit)
    high_ref[0] = jax.nn.sigmoid(high)
    low_ref[0] = jax.nn.sigmoid(low)

    for copy in (to_right, to_left, to_down, to_up, *level_copies):
        copy.wait_send()


def on_device(mask, kernels, socs_weight, dose, threshold):
    core = mask.shape[1]
    conds, kerns, band = kernels.shape[:3]
    tables = [jnp.asarray(t) for t in make_tables(core, band)]
    count = (core + 2 * MARGIN) // STEP
    smem = pl.BlockSpec(memory_space=pltpu.SMEM)
    anywhere = pl.BlockSpec(memory_space=pl.ANY)
    vmem = pl.BlockSpec(memory_space=pltpu.VMEM)
    loads = 1 + len(tables) + conds
    out = jax.ShapeDtypeStruct((1, core // 2, core), jnp.float32)
    return pl.pallas_call(
        functools.partial(kernel, lax.axis_size("tile")),
        out_shape=(out, out),
        in_specs=[smem] * 3 + [anywhere] * (2 + len(tables)),
        out_specs=(vmem, vmem),
        scratch_shapes=[
            pltpu.VMEM(mask.shape[1:], mask.dtype),
            pltpu.VMEM(kernels.shape, kernels.dtype),
            *[pltpu.VMEM(t.shape, t.dtype) for t in tables],
            pltpu.VMEM((core, LANES), mask.dtype),
            pltpu.VMEM((core, LANES), mask.dtype),
            pltpu.VMEM((core, 2 * band), jnp.bfloat16),
            pltpu.VMEM((2 * MARGIN, 2 * band), jnp.bfloat16),
            pltpu.VMEM((conds, count, count), jnp.float32),
            pltpu.VMEM((conds, count, count), jnp.float32),
            pltpu.SemaphoreType.DMA((loads,)),
            pltpu.SemaphoreType.DMA((4,)),
            pltpu.SemaphoreType.DMA((4,)),
            pltpu.SemaphoreType.DMA((conds,)),
            pltpu.SemaphoreType.DMA((conds,)),
        ],
        compiler_params=pltpu.CompilerParams(collective_id=0, has_side_effects=True),
        name="expose",
    )(socs_weight, dose, threshold, mask, kernels, *tables)


def solution(mesh):
    return jax.shard_map(
        on_device,
        mesh=mesh,
        in_specs=(
            P(("parts", "tile"), None, None),
            P("cond", None, None, None),
            P("cond", None),
            P("cond"),
            P("cond"),
        ),
        out_specs=(P(("parts", "tile"), "cond", None), P(("parts", "tile"), "cond", None)),
        check_vma=False,
    )
```

time: 240 us -> 78.6 us (0.33)
  matrix products: 78.9 us -> 0 us
  Pallas kernels: 0 us -> 74.6 us
  starting transfers between devices: 59 us -> 0 us
  local copies, waits for them, and re-layouts: 61 us -> 3.14 us
  other arithmetic: 21.5 us -> 0 us
  waiting for transfers between devices: 9.7 us -> 0 us
  blocking collectives: 6.44 us -> 0 us
    dot_general x118 -> x0, matrix products: 78.9 us -> none  [the longest x4 15.6 us: expose(): blurred = jnp.dot(jnp.dot(blur_rows, intensity), blur_rows.T)]
    pallas_call x0 -> x1, Pallas kernels: none -> 74.6 us  [on_device(): pl.pallas_call(functools.partial(kernel, lax.axis_size('tile')), out_shap...]
    ppermute x4 -> x0, starting transfers between devices: 59 us -> none  [shifted(): return lax.ppermute(block, axis, route)]
    add x12 -> x0, local copies, waits for them, and re-layouts: 24.6 us -> none  [group_power(): power = field_real * field_real + field_imag * field_imag]
    dynamic_slice x12 -> x0, local copies, waits for them, and re-layouts: 14.3 us -> none  [on_device(): resist = lax.map(one_condition, (kernels, socs_weight, dose, threshold))]
    reduce_sum x9 -> x0, other arithmetic: 11.8 us -> none  [the longest x4 5.69 us: expose(): jnp.sum(lax.map(group_power, (kernel_groups, weight_groups)), axis=0)]
    squeeze x12 -> x0, local copies, waits for them, and re-layouts: 11 us -> none  [expose(): lax.map(group_power, (kernel_groups, weight_groups))]
    ppermute x4 -> x0, waiting for transfers between devices: 9.7 us -> none  [shifted(): return lax.ppermute(block, axis, route)]
  transfers between devices with their start and end apart: 4 -> 0, of which waited for: 2 -> 0; matrix products, arithmetic and copies ran while one was open for 0% -> 0% of each run, Pallas kernels for 0% -> 0%
where the time goes in v1:
time: 78.6 us; the launch traced here: 78.4 us
  Pallas kernels  74.6 us (95%)
  local copies, waits for them, and re-layouts  3.14 us (4%)
    pallas_call x1, Pallas kernels, on_device(): pl.pallas_call(functools.partial(kernel, lax.axis_size('tile')), out_shap...  74.6 us
    unnamed x2, local copies, waits for them, and re-layouts  3.14 us

profile of v1, /device:TPU:65, one launch (start us, length us, event | category | flops | bytes accessed | tf_op | source)
XLA Modules:
  0.0 78.4 jit_solution(14216463590804465038)
XLA Ops:
  0.6 74.6 %expose.1 = (f32[1,128,256]{2,1,0:T(8,128)}, f32[1,128,256]{2,1,0:T(8,128)}) custom-call(f32[4,24]{1,0:T(4,128)} %weight_ref.1, f32[4]{0:T(128)} %dose_ref.1, f32[4]{0:T(128)} %threshold_ref.1, bf16[1,256,256]{2,1,0:T(8,128)(2,1)} %mask_hbm.1, bf16[4,24,64,128]{3,2,1,0:T(8,128)(2,1)} %kernels_hbm.1, bf16[512,128]{1,0:T(8,128)(2,1)} %constant.14.clone.columns_hbm, ...), custom_call_target="tpu_custom_call" | custom-call | tf_op jit(solution)/shard_map/expose/pallas_call | solution.py:288
  75.2 1.6 %copy.16 = f32[1,128,256]{2,1,0:T(8,128)} copy(f32[1,128,256]{2,1,0:T(8,128)} %get-tuple-element.4) | data formatting | bytes 262144
  76.8 1.6 %copy.17 = f32[1,128,256]{2,1,0:T(8,128)} copy(f32[1,128,256]{2,1,0:T(8,128)} %get-tuple-element.5) | data formatting | bytes 262144

commit v2 on v1

v2 whole, which is shorter than its diff:
```python
import functools

import jax
import jax.numpy as jnp
import numpy as np
from jax import lax
from jax.experimental import pallas as pl
from jax.experimental.pallas import tpu as pltpu
from jax.sharding import PartitionSpec as P

MESH = pl.DeviceIdType.MESH
MARGIN = 64
BLUR = 8
LANES = 128
STEP = 3
PACK = 4
GROUP = 8

diffusion = 2.0
steepness = 8.0


def phase(pixels, pad_width, band_width):
    freq = np.arange(band_width) - band_width // 2
    angle = 2.0 * np.pi * ((pixels[:, None] * freq[None, :]) % pad_width) / pad_width
    return np.cos(angle), np.sin(angle)


def make_tables(core, band_width):
    pad_width = core + 2 * MARGIN
    bf16 = lambda a: np.asarray(a, np.float32).astype(jnp.bfloat16)
    cos_in, sin_in = phase(np.arange(pad_width), pad_width, band_width)
    both = np.concatenate([cos_in, -sin_in], axis=1)
    columns = both[MARGIN : MARGIN + core]
    nil = np.zeros((MARGIN, 2 * band_width))
    strips = []
    for strip in (both[:MARGIN], both[MARGIN + core :]):
        strips.append(np.block([[strip, nil], [nil, strip]]))
    rows = np.concatenate([cos_in.T, sin_in.T], axis=0)
    own_rows = rows[:, MARGIN : MARGIN + core]
    far_rows = np.concatenate([rows[:, :MARGIN], rows[:, MARGIN + core :]], axis=1)
    count = pad_width // STEP
    cos_s, sin_s = phase(np.arange(count) * STEP, pad_width, band_width)
    first = np.block([[cos_s, -sin_s, -sin_s, cos_s], [sin_s, cos_s, cos_s, sin_s]])
    nil = np.zeros((band_width, count))
    second = np.block(
        [
            [cos_s.T, sin_s.T, nil, nil],
            [nil, nil, cos_s.T, sin_s.T],
            [-sin_s.T, cos_s.T, nil, nil],
            [nil, nil, -sin_s.T, cos_s.T],
        ]
    )
    offset = np.arange(core + 2 * BLUR)[None, :] - np.arange(core)[:, None] - BLUR
    taps = np.where(np.abs(offset) <= BLUR, np.exp(-(offset**2) / (2.0 * diffusion**2)), 0.0)
    reach = np.arange(-BLUR, BLUR + 1)
    taps = taps / np.sum(np.exp(-(reach**2) / (2.0 * diffusion**2)))
    pixel = np.arange(MARGIN - BLUR, MARGIN + core + BLUR)
    wave = np.arange(-(band_width - 1), band_width)
    apart = pixel[:, None] - STEP * np.arange(count)[None, :]
    interpolate = np.cos(2.0 * np.pi * apart[:, :, None] * wave / pad_width).sum(-1) / count
    smooth = np.asarray(taps @ interpolate, np.float32)
    high = bf16(smooth).astype(np.float32)
    low = smooth - high
    rows_out = np.concatenate([high, low, high], axis=1)
    cols_out = np.concatenate([high.T, low.T, high.T], axis=0)
    rows_out = rows_out.reshape(2, core // 2, 3 * count)
    return tuple(
        bf16(a) for a in (columns, np.stack(strips), own_rows, far_rows, first, second, rows_out, cols_out)
    )


def nt_dot(a, b):
    return lax.dot_general(a, b, (((1,), (1,)), ((), ())), preferred_element_type=jnp.float32)


def dot(a, b):
    return jnp.dot(a, b, preferred_element_type=jnp.float32)


def halves(a):
    high = a.astype(jnp.bfloat16)
    return high, (a - high.astype(jnp.float32)).astype(jnp.bfloat16)


def spot(tiles):
    grid_cols = min(8, tiles // 2)
    place = lax.rem(lax.axis_index("tile") + grid_cols // 2, tiles)
    column = lax.rem(place, grid_cols)
    row = lax.div(place, grid_cols)
    odd = lax.rem(row, 2) == 1
    seam_left = jnp.logical_and(odd, column == grid_cols // 2)
    seam_right = jnp.logical_and(odd, column == grid_cols // 2 - 1)
    return grid_cols, column, row, seam_left, seam_right


def last_columns(mask_v):
    rows, columns = mask_v.shape
    upper = mask_v[: rows // 2, columns - LANES :].astype(jnp.float32)
    lower = mask_v[rows // 2 :, columns - LANES :].astype(jnp.float32)
    early = lax.broadcasted_iota(jnp.int32, upper.shape, 1) < MARGIN
    return jnp.where(early, pltpu.roll(upper, MARGIN, axis=1), lower).astype(mask_v.dtype)


def first_columns(mask_v):
    rows = mask_v.shape[0]
    upper = mask_v[: rows // 2, :LANES].astype(jnp.float32)
    lower = mask_v[rows // 2 :, :LANES].astype(jnp.float32)
    early = lax.broadcasted_iota(jnp.int32, upper.shape, 1) < MARGIN
    return jnp.where(early, upper, pltpu.roll(lower, MARGIN, axis=1)).astype(mask_v.dtype)


def seam_kernel(tiles, mask_hbm, strip_hbm, mask_v, packed_v, load_sem, send_sem, recv_sem):
    tile = lax.axis_index("tile")
    _, _, _, seam_left, seam_right = spot(tiles)

    def exchange(peer, pack):
        barrier = pltpu.get_barrier_semaphore()
        pl.semaphore_signal(barrier, inc=1, device_id=peer, device_id_type=MESH)
        load = pltpu.make_async_copy(mask_hbm.at[0], mask_v, load_sem)
        load.start()
        load.wait()
        packed_v[...] = pack(mask_v)
        pl.semaphore_wait(barrier, 1)
        copy = pltpu.make_async_remote_copy(
            src_ref=packed_v,
            dst_ref=strip_hbm,
            send_sem=send_sem,
            recv_sem=recv_sem,
            device_id=peer,
            device_id_type=MESH,
        )
        copy.start()
        copy.wait()

    @pl.when(seam_right)
    def _():
        exchange({"tile": lax.rem(tile + 1, tiles)}, last_columns)

    @pl.when(seam_left)
    def _():
        exchange({"tile": lax.rem(tile + tiles - 1, tiles)}, first_columns)


def kernel(
    tiles,
    weight_hbm,
    dose_ref,
    threshold_ref,
    mask_hbm,
    kernels_hbm,
    strip_hbm,
    columns_hbm,
    strips_hbm,
    own_rows_hbm,
    far_rows_hbm,
    first_hbm,
    second_hbm,
    rows_out_hbm,
    cols_out_hbm,
    high_ref,
    low_ref,
    weight_ref,
    mask_v,
    kernels_v,
    columns_v,
    strips_v,
    own_rows_v,
    far_rows_v,
    first_v,
    second_v,
    rows_out_v,
    cols_out_v,
    packed_v,
    left_v,
    right_v,
    spec_rows,
    far_v,
    pair_v,
    own_level,
    sib_level,
    load_sem,
    strip_sem,
    send_sem,
    recv_sem,
    level_send,
    level_recv,
):
    conds, kerns, band = kernels_v.shape[:3]
    core = mask_v.shape[0]
    half = core // 2
    count = own_level.shape[1]
    tile = lax.axis_index("tile")
    cond = lax.axis_index("cond")
    grid_cols, column, row, seam_left, seam_right = spot(tiles)
    has_left = column > 0
    has_right = column < grid_cols - 1
    has_up = row > 0
    has_down = row < tiles // grid_cols - 1
    greet_left = jnp.logical_and(has_left, jnp.logical_not(seam_left))
    greet_right = jnp.logical_and(has_right, jnp.logical_not(seam_right))
    right = {"tile": lax.rem(tile + 1, tiles)}
    left = {"tile": lax.rem(tile + tiles - 1, tiles)}
    down = {"tile": lax.rem(tile + grid_cols, tiles)}
    up = {"tile": lax.rem(tile + tiles - grid_cols, tiles)}
    sibling = {"cond": 1 - cond}

    barrier = pltpu.get_barrier_semaphore()
    peers = 1
    for flag, peer in ((has_up, up), (has_down, down), (greet_left, left), (greet_right, right)):
        peers = peers + flag.astype(jnp.int32)

        @pl.when(flag)
        def _(peer=peer):
            pl.semaphore_signal(barrier, inc=1, device_id=peer, device_id_type=MESH)

    pl.semaphore_signal(barrier, inc=1, device_id=sibling, device_id_type=MESH)

    sources = (
        mask_hbm.at[0],
        columns_hbm,
        strips_hbm,
        own_rows_hbm,
        far_rows_hbm,
        first_hbm,
        second_hbm,
        weight_hbm,
        rows_out_hbm,
        cols_out_hbm,
        *[kernels_hbm.at[c] for c in range(conds)],
    )
    targets = (
        mask_v,
        columns_v,
        strips_v,
        own_rows_v,
        far_rows_v,
        first_v,
        second_v,
        weight_ref,
        rows_out_v,
        cols_out_v,
        *[kernels_v.at[c] for c in range(conds)],
    )
    loads = [
        pltpu.make_async_copy(s, t, load_sem.at[i]) for i, (s, t) in enumerate(zip(sources, targets))
    ]
    for load in loads:
        load.start()
    from_seam = [
        (seam_left, pltpu.make_async_copy(strip_hbm, left_v, strip_sem)),
        (seam_right, pltpu.make_async_copy(strip_hbm, right_v, strip_sem)),
    ]
    for flag, copy in from_seam:
        pl.when(flag)(copy.start)

    def remote(src, dst, i, peer):
        return pltpu.make_async_remote_copy(
            src_ref=src,
            dst_ref=dst,
            send_sem=send_sem.at[i],
            recv_sem=recv_sem.at[i],
            device_id=peer,
            device_id_type=MESH,
        )

    to_right = remote(packed_v.at[0], left_v, 0, right)
    to_left = remote(packed_v.at[1], right_v, 1, left)
    to_down = remote(spec_rows.at[core - MARGIN :], far_v.at[:MARGIN], 2, down)
    to_up = remote(spec_rows.at[:MARGIN], far_v.at[MARGIN:], 3, up)

    loads[0].wait()
    packed_v[0] = last_columns(mask_v)
    packed_v[1] = first_columns(mask_v)
    pl.semaphore_wait(barrier, peers)
    pl.when(greet_right)(to_right.start)
    pl.when(greet_left)(to_left.start)

    for load in loads[1:]:
        load.wait()
    part = dot(mask_v[...], columns_v[...])
    zero = jnp.zeros((half, LANES), jnp.bfloat16)
    pl.when(seam_left)(from_seam[0][1].wait)
    pl.when(seam_right)(from_seam[1][1].wait)
    pl.when(greet_left)(to_right.wait_recv)
    pl.when(greet_right)(to_left.wait_recv)
    aside = dot(jnp.where(has_left, left_v[...], zero), strips_v[0])
    aside += dot(jnp.where(has_right, right_v[...], zero), strips_v[1])
    spec_rows[:half] = (part[:half] + aside[:, : 2 * band]).astype(jnp.bfloat16)
    spec_rows[half:] = (part[half:] + aside[:, 2 * band :]).astype(jnp.bfloat16)
    pl.when(has_down)(to_down.start)
    pl.when(has_up)(to_up.start)
    mixed = dot(own_rows_v[...], spec_rows[...])
    pl.when(has_up)(to_down.wait_recv)
    pl.when(has_down)(to_up.wait_recv)
    zero = jnp.zeros((MARGIN, 2 * band), jnp.bfloat16)
    above = jnp.where(has_up, far_v[:MARGIN], zero)
    below = jnp.where(has_down, far_v[MARGIN:], zero)
    mixed += dot(far_rows_v[...], jnp.concatenate([above, below], axis=0))
    mixed *= 1.0 / ((core + 2 * MARGIN) * band)
    lower = lax.broadcasted_iota(jnp.int32, (band, 2 * band), 1) < band
    turned = pltpu.roll(mixed[band:], band, axis=1)
    spec = mixed[:band] + jnp.where(lower, turned, -turned)
    swapped = pltpu.roll(spec, band, axis=1)
    reals = jnp.where(lower, spec, swapped)
    imags = jnp.where(lower, swapped, -spec)

    steps = kerns // GROUP

    def first_half(s):
        c, g = divmod(s, steps)
        for i in range(GROUP // PACK):
            rows = []
            for j in range(PACK):
                held = kernels_v[c, g * GROUP + i * PACK + j].astype(jnp.float32)
                rows.append(
                    jnp.concatenate(
                        [(reals * held).astype(jnp.bfloat16), (imags * held).astype(jnp.bfloat16)],
                        axis=1,
                    )
                )
            out = nt_dot(first_v[...], jnp.concatenate(rows, axis=0)).astype(jnp.bfloat16)
            for j in range(PACK // 2):
                span = slice(j * 2 * band, (j + 1) * 2 * band)
                at = i * (PACK // 2) + j
                pair_v[s % 2, at * count : (at + 1) * count, : 2 * band] = out[:count, span]
                pair_v[s % 2, at * count : (at + 1) * count, 2 * band :] = out[count:, span]

    def second_half(s, level):
        c, g = divmod(s, steps)
        field = dot(pair_v[s % 2], second_v[...])
        for at in range(GROUP // 2):
            for i in range(2):
                re = field[at * count : (at + 1) * count, 2 * i * count : (2 * i + 1) * count]
                im = field[at * count : (at + 1) * count, (2 * i + 1) * count : (2 * i + 2) * count]
                term = weight_ref[c, g * GROUP + 2 * at + i] * (re * re + im * im)
                level = term if level is None else level + term
        return level

    rows_out = rows_out_v[cond]
    bounds = []

    def blur(level):
        fine, rest = halves(level)
        tall = nt_dot(rows_out, jnp.concatenate([fine, fine, rest], axis=1))
        fine, rest = halves(tall)
        logit = dot(jnp.concatenate([fine, fine, rest], axis=1), cols_out_v[...])
        if bounds:
            bounds[0] = jnp.maximum(bounds[0], logit)
            bounds[1] = jnp.minimum(bounds[1], logit)
        else:
            bounds.extend([logit, logit])

    level_copies = []
    first_half(0)
    level = None
    for s in range(conds * steps):
        c = s // steps
        if s + 1 < conds * steps:
            first_half(s + 1)
        level = second_half(s, level)
        if s % steps == steps - 1:
            total = weight_ref[c, 0]
            for k in range(1, kerns):
                total += weight_ref[c, k]
            scale = jnp.full((1, count), steepness * dose_ref[c]) / jnp.full((1, count), total)
            own_level[c] = level * scale - steepness * threshold_ref[c]
            copy = pltpu.make_async_remote_copy(
                src_ref=own_level.at[c],
                dst_ref=sib_level.at[c],
                send_sem=level_send.at[c],
                recv_sem=level_recv.at[c],
                device_id=sibling,
                device_id_type=MESH,
            )
            copy.start()
            level_copies.append(copy)
            level = None
            blur(own_level[c])
            if c > 0:
                level_copies[c - 1].wait_recv()
                blur(sib_level[c - 1])
    level_copies[-1].wait_recv()
    blur(sib_level[conds - 1])
    high_ref[0] = jax.nn.sigmoid(bounds[0])
    low_ref[0] = jax.nn.sigmoid(bounds[1])

    for flag, copy in (
        (greet_right, to_right),
        (greet_left, to_left),
        (has_down, to_down),
        (has_up, to_up),
    ):
        pl.when(flag)(copy.wait_send)
    for copy in level_copies:
        copy.wait_send()


def store_kernel(high_ref, low_ref, high_out, low_out, sem):
    copies = [
        pltpu.make_async_copy(high_ref, high_out, sem.at[0]),
        pltpu.make_async_copy(low_ref, low_out, sem.at[1]),
    ]
    for copy in copies:
        copy.start()
    for copy in copies:
        copy.wait()


def on_device(mask, kernels, socs_weight, dose, threshold):
    core = mask.shape[1]
    conds, kerns, band = kernels.shape[:3]
    tiles = lax.axis_size("tile")
    tables = [jnp.asarray(t) for t in make_tables(core, band)]
    count = (core + 2 * MARGIN) // STEP
    smem = pl.BlockSpec(memory_space=pltpu.SMEM)
    anywhere = pl.BlockSpec(memory_space=pl.ANY)
    vmem = pl.BlockSpec(memory_space=pltpu.VMEM)
    strip = (core // 2, LANES)
    seam = pl.pallas_call(
        functools.partial(seam_kernel, tiles),
        out_shape=jax.ShapeDtypeStruct(strip, mask.dtype),
        in_specs=[anywhere],
        out_specs=anywhere,
        scratch_shapes=[
            pltpu.VMEM(mask.shape[1:], mask.dtype),
            pltpu.VMEM(strip, mask.dtype),
            pltpu.SemaphoreType.DMA,
            pltpu.SemaphoreType.DMA,
            pltpu.SemaphoreType.DMA,
        ],
        compiler_params=pltpu.CompilerParams(collective_id=1, has_side_effects=True),
        name="seam",
    )(mask)
    loads = 2 + len(tables) + conds
    out = pltpu.VMEM((1, core // 2, core), jnp.float32)
    results = pl.pallas_call(
        functools.partial(kernel, tiles),
        out_shape=(out, out),
        in_specs=[anywhere, smem, smem] + [anywhere] * (3 + len(tables)),
        out_specs=(vmem, vmem),
        scratch_shapes=[
            pltpu.SMEM(socs_weight.shape, jnp.float32),
            pltpu.VMEM(mask.shape[1:], mask.dtype),
            pltpu.VMEM(kernels.shape, kernels.dtype),
            *[pltpu.VMEM(t.shape, t.dtype) for t in tables],
            pltpu.VMEM((2, *strip), mask.dtype),
            pltpu.VMEM(strip, mask.dtype),
            pltpu.VMEM(strip, mask.dtype),
            pltpu.VMEM((core, 2 * band), jnp.bfloat16),
            pltpu.VMEM((2 * MARGIN, 2 * band), jnp.bfloat16),
            pltpu.VMEM((2, GROUP // 2 * count, 4 * band), jnp.bfloat16),
            pltpu.VMEM((conds, count, count), jnp.float32),
            pltpu.VMEM((conds, count, count), jnp.float32),
            pltpu.SemaphoreType.DMA((loads,)),
            pltpu.SemaphoreType.DMA,
            pltpu.SemaphoreType.DMA((4,)),
            pltpu.SemaphoreType.DMA((4,)),
            pltpu.SemaphoreType.DMA((conds,)),
            pltpu.SemaphoreType.DMA((conds,)),
        ],
        compiler_params=pltpu.CompilerParams(collective_id=0, has_side_effects=True),
        name="expose",
    )(socs_weight, dose, threshold, mask, kernels, seam, *tables)
    final = jax.ShapeDtypeStruct((1, core // 2, core), jnp.float32)
    return pl.pallas_call(
        store_kernel,
        out_shape=(final, final),
        in_specs=[vmem, vmem],
        out_specs=(anywhere, anywhere),
        scratch_shapes=[pltpu.SemaphoreType.DMA((2,))],
        name="store",
    )(*(pltpu.with_memory_space_constraint(r, pltpu.VMEM) for r in results))


def solution(mesh):
    return jax.shard_map(
        on_device,
        mesh=mesh,
        in_specs=(
            P(("parts", "tile"), None, None),
            P("cond", None, None, None),
            P("cond", None),
            P("cond"),
            P("cond"),
        ),
        out_specs=(P(("parts", "tile"), "cond", None), P(("parts", "tile"), "cond", None)),
        check_vma=False,
    )
```

time: 78.6 us -> 64.7 us (0.82)
  Pallas kernels: 74.6 us -> 63.8 us
  local copies, waits for them, and re-layouts: 3.14 us -> 0 us
    pallas_call x1 -> x3, Pallas kernels: 74.6 us -> 63.8 us  [the longest x1 62.4 us: on_device(): pl.pallas_call(functools.partial(kernel, tiles), out_shape=(out, out), in...]
    unnamed x2 -> x0, local copies, waits for them, and re-layouts: 3.14 us -> none
where the time goes in v2:
time: 64.7 us; the launch traced here: 64.5 us
  Pallas kernels  63.8 us (99%)
    pallas_call x1, Pallas kernels, on_device(): pl.pallas_call(functools.partial(kernel, tiles), out_shape=(out, out), in...  62.4 us

profile of v2, /device:TPU:65, one launch (start us, length us, event | category | flops | bytes accessed | tf_op | source)
XLA Modules:
  0.0 64.5 jit_solution(11391014474707885456)
XLA Ops:
  0.6 0.7 %seam.1.strip_hbm = bf16[128,128]{1,0:T(8,128)(2,1)} custom-call(bf16[1,256,256]{2,1,0:T(8,128)(2,1)} %mask_hbm.3), custom_call_target="tpu_custom_call" | custom-call | tf_op jit(solution)/shard_map/seam/pallas_call | solution.py:420
  1.4 62.4 %expose.1 = (f32[1,128,256]{2,1,0:T(8,128)S(1)}, f32[1,128,256]{2,1,0:T(8,128)S(1)}) custom-call(f32[4,24]{1,0:T(4,128)} %weight_hbm.1, f32[4]{0:T(128)} %dose_ref.1, f32[4]{0:T(128)} %threshold_ref.1, bf16[1,256,256]{2,1,0:T(8,128)(2,1)} %mask_hbm.3, bf16[4,24,64,128]{3,2,1,0:T(8,128)(2,1)} %kernels_hbm.1, bf16[128,128]{1,0:T(8,128)(2,1)} %seam.1.strip_hbm, ...), custom_call_target="tpu_custom_call" | custom-call | tf_op jit(solution)/shard_map/expose/pallas_call | solution.py:437
  63.8 0.7 %store.1 = (f32[1,128,256]{2,1,0:T(8,128)}, f32[1,128,256]{2,1,0:T(8,128)}) custom-call(f32[1,128,256]{2,1,0:T(8,128)S(1)} %get-tuple-element.4.high_ref, f32[1,128,256]{2,1,0:T(8,128)S(1)} %get-tuple-element.5.low_ref), custom_call_target="tpu_custom_call" | custom-call | tf_op jit(solution)/shard_map/store/pallas_call | solution.py:466

commit v3 on v2

--- a/solution.py
+++ b/solution.py
@@ -24,6 +24,20 @@
     freq = np.arange(band_width) - band_width // 2
     angle = 2.0 * np.pi * ((pixels[:, None] * freq[None, :]) % pad_width) / pad_width
     return np.cos(angle), np.sin(angle)
+
+
+def rounded_rows(exact):
+    out = exact.astype(jnp.bfloat16).astype(np.float64)
+    for row in out:
+        for _ in range(64):
+            excess = row.sum() - 1.0
+            toward = np.full(row.shape, -np.inf if excess > 0 else np.inf).astype(jnp.bfloat16)
+            moved = np.nextafter(row.astype(jnp.bfloat16), toward).astype(np.float64)
+            left = np.abs(excess + moved - row)
+            if excess == 0 or left.min() >= abs(excess):
+                break
+            row[left.argmin()] = moved[left.argmin()]
+    return out
 
 
 def make_tables(core, band_width):
@@ -59,12 +73,11 @@
     wave = np.arange(-(band_width - 1), band_width)
     apart = pixel[:, None] - STEP * np.arange(count)[None, :]
     interpolate = np.cos(2.0 * np.pi * apart[:, :, None] * wave / pad_width).sum(-1) / count
-    smooth = np.asarray(taps @ interpolate, np.float32)
-    high = bf16(smooth).astype(np.float32)
-    low = smooth - high
-    rows_out = np.concatenate([high, low, high], axis=1)
-    cols_out = np.concatenate([high.T, low.T, high.T], axis=0)
-    rows_out = rows_out.reshape(2, core // 2, 3 * count)
+    smooth = taps @ interpolate
+    smooth = rounded_rows(smooth)
+    rows_out = np.concatenate([smooth, smooth], axis=1)
+    cols_out = rows_out.T
+    rows_out = rows_out.reshape(2, core // 2, 2 * count)
     return tuple(
         bf16(a) for a in (columns, np.stack(strips), own_rows, far_rows, first, second, rows_out, cols_out)
     )
@@ -145,8 +158,8 @@
 def kernel(
     tiles,
     weight_hbm,
-    dose_ref,
-    threshold_ref,
+    dose_hbm,
+    threshold_hbm,
     mask_hbm,
     kernels_hbm,
     strip_hbm,
@@ -161,6 +174,8 @@
     high_ref,
     low_ref,
     weight_ref,
+    dose_ref,
+    threshold_ref,
     mask_v,
     kernels_v,
     columns_v,
@@ -201,20 +216,12 @@
     greet_right = jnp.logical_and(has_right, jnp.logical_not(seam_right))
     right = {"tile": lax.rem(tile + 1, tiles)}
     left = {"tile": lax.rem(tile + tiles - 1, tiles)}
-    down = {"tile": lax.rem(tile + grid_cols, tiles)}
-    up = {"tile": lax.rem(tile + tiles - grid_cols, tiles)}
+    far = {"tile": lax.rem(tile + tiles + grid_cols * (2 * cond - 1), tiles), "cond": 1 - cond}
+    far_row = row + 2 * cond - 1
+    has_far = jnp.logical_and(far_row >= 0, far_row < tiles // grid_cols)
+    other_row = row + 1 - 2 * cond
+    has_other = jnp.logical_and(other_row >= 0, other_row < tiles // grid_cols)
     sibling = {"cond": 1 - cond}
-
-    barrier = pltpu.get_barrier_semaphore()
-    peers = 1
-    for flag, peer in ((has_up, up), (has_down, down), (greet_left, left), (greet_right, right)):
-        peers = peers + flag.astype(jnp.int32)
-
-        @pl.when(flag)
-        def _(peer=peer):
-            pl.semaphore_signal(barrier, inc=1, device_id=peer, device_id_type=MESH)
-
-    pl.semaphore_signal(barrier, inc=1, device_id=sibling, device_id_type=MESH)
 
     sources = (
         mask_hbm.at[0],
@@ -225,6 +232,8 @@
         first_hbm,
         second_hbm,
         weight_hbm,
+        dose_hbm,
+        threshold_hbm,
         rows_out_hbm,
         cols_out_hbm,
         *[kernels_hbm.at[c] for c in range(conds)],
@@ -238,6 +247,8 @@
         first_v,
         second_v,
         weight_ref,
+        dose_ref,
+        threshold_ref,
         rows_out_v,
         cols_out_v,
         *[kernels_v.at[c] for c in range(conds)],
@@ -245,7 +256,18 @@
     loads = [
         pltpu.make_async_copy(s, t, load_sem.at[i]) for i, (s, t) in enumerate(zip(sources, targets))
     ]
-    for load in loads:
+    loads[0].start()
+    barrier = pltpu.get_barrier_semaphore()
+    peers = 1
+    for flag, peer in ((has_far, far), (greet_left, left), (greet_right, right)):
+        peers = peers + flag.astype(jnp.int32)
+
+        @pl.when(flag)
+        def _(peer=peer):
+            pl.semaphore_signal(barrier, inc=1, device_id=peer, device_id_type=MESH)
+
+    pl.semaphore_signal(barrier, inc=1, device_id=sibling, device_id_type=MESH)
+    for load in loads[1:]:
         load.start()
     from_seam = [
         (seam_left, pltpu.make_async_copy(strip_hbm, left_v, strip_sem)),
@@ -266,8 +288,10 @@
 
     to_right = remote(packed_v.at[0], left_v, 0, right)
     to_left = remote(packed_v.at[1], right_v, 1, left)
-    to_down = remote(spec_rows.at[core - MARGIN :], far_v.at[:MARGIN], 2, down)
-    to_up = remote(spec_rows.at[:MARGIN], far_v.at[MARGIN:], 3, up)
+    edge = pl.ds(pl.multiple_of(cond * (core - MARGIN), MARGIN), MARGIN)
+    to_far = remote(spec_rows.at[edge], far_v.at[1 - cond], 2, far)
+    to_sibling = remote(far_v.at[cond], far_v.at[cond], 3, sibling)
+    from_sibling = remote(far_v.at[1 - cond], far_v.at[1 - cond], 3, sibling)
 
     loads[0].wait()
     packed_v[0] = last_columns(mask_v)
@@ -288,14 +312,18 @@
     aside += dot(jnp.where(has_right, right_v[...], zero), strips_v[1])
     spec_rows[:half] = (part[:half] + aside[:, : 2 * band]).astype(jnp.bfloat16)
     spec_rows[half:] = (part[half:] + aside[:, 2 * band :]).astype(jnp.bfloat16)
-    pl.when(has_down)(to_down.start)
-    pl.when(has_up)(to_up.start)
+    pl.when(has_far)(to_far.start)
     mixed = dot(own_rows_v[...], spec_rows[...])
-    pl.when(has_up)(to_down.wait_recv)
-    pl.when(has_down)(to_up.wait_recv)
+
+    @pl.when(has_far)
+    def _():
+        to_far.wait_recv()
+        to_sibling.start()
+
+    pl.when(has_other)(from_sibling.wait_recv)
     zero = jnp.zeros((MARGIN, 2 * band), jnp.bfloat16)
-    above = jnp.where(has_up, far_v[:MARGIN], zero)
-    below = jnp.where(has_down, far_v[MARGIN:], zero)
+    above = jnp.where(has_up, far_v[0], zero)
+    below = jnp.where(has_down, far_v[1], zero)
     mixed += dot(far_rows_v[...], jnp.concatenate([above, below], axis=0))
     mixed *= 1.0 / ((core + 2 * MARGIN) * band)
     lower = lax.broadcasted_iota(jnp.int32, (band, 2 * band), 1) < band
@@ -342,9 +370,9 @@
 
     def blur(level):
         fine, rest = halves(level)
-        tall = nt_dot(rows_out, jnp.concatenate([fine, fine, rest], axis=1))
+        tall = nt_dot(rows_out, jnp.concatenate([fine, rest], axis=1))
         fine, rest = halves(tall)
-        logit = dot(jnp.concatenate([fine, fine, rest], axis=1), cols_out_v[...])
+        logit = dot(jnp.concatenate([fine, rest], axis=1), cols_out_v[...])
         if bounds:
             bounds[0] = jnp.maximum(bounds[0], logit)
             bounds[1] = jnp.minimum(bounds[1], logit)
@@ -352,6 +380,7 @@
             bounds.extend([logit, logit])
 
     level_copies = []
+    ready = []
     first_half(0)
     level = None
     for s in range(conds * steps):
@@ -360,6 +389,9 @@
             first_half(s + 1)
         level = second_half(s, level)
         if s % steps == steps - 1:
+            for ref in ready:
+                blur(ref[...])
+            ready = [own_level.at[c]]
             total = weight_ref[c, 0]
             for k in range(1, kerns):
                 total += weight_ref[c, k]
@@ -376,10 +408,11 @@
             copy.start()
             level_copies.append(copy)
             level = None
-            blur(own_level[c])
             if c > 0:
                 level_copies[c - 1].wait_recv()
-                blur(sib_level[c - 1])
+                ready.append(sib_level.at[c - 1])
+    for ref in ready:
+        blur(ref[...])
     level_copies[-1].wait_recv()
     blur(sib_level[conds - 1])
     high_ref[0] = jax.nn.sigmoid(bounds[0])
@@ -388,8 +421,8 @@
     for flag, copy in (
         (greet_right, to_right),
         (greet_left, to_left),
-        (has_down, to_down),
-        (has_up, to_up),
+        (has_far, to_far),
+        (has_far, to_sibling),
     ):
         pl.when(flag)(copy.wait_send)
     for copy in level_copies:
@@ -413,7 +446,6 @@
     tiles = lax.axis_size("tile")
     tables = [jnp.asarray(t) for t in make_tables(core, band)]
     count = (core + 2 * MARGIN) // STEP
-    smem = pl.BlockSpec(memory_space=pltpu.SMEM)
     anywhere = pl.BlockSpec(memory_space=pl.ANY)
     vmem = pl.BlockSpec(memory_space=pltpu.VMEM)
     strip = (core // 2, LANES)
@@ -432,15 +464,15 @@
         compiler_params=pltpu.CompilerParams(collective_id=1, has_side_effects=True),
         name="seam",
     )(mask)
-    loads = 2 + len(tables) + conds
+    loads = 4 + len(tables) + conds
     out = pltpu.VMEM((1, core // 2, core), jnp.float32)
     results = pl.pallas_call(
         functools.partial(kernel, tiles),
         out_shape=(out, out),
-        in_specs=[anywhere, smem, smem] + [anywhere] * (3 + len(tables)),
+        in_specs=[anywhere] * (6 + len(tables)),
         out_specs=(vmem, vmem),
         scratch_shapes=[
-            pltpu.SMEM(socs_weight.shape, jnp.float32),
+            *[pltpu.SMEM(a.shape, a.dtype) for a in (socs_weight, dose, threshold)],
             pltpu.VMEM(mask.shape[1:], mask.dtype),
             pltpu.VMEM(kernels.shape, kernels.dtype),
             *[pltpu.VMEM(t.shape, t.dtype) for t in tables],
@@ -448,7 +480,7 @@
             pltpu.VMEM(strip, mask.dtype),
             pltpu.VMEM(strip, mask.dtype),
             pltpu.VMEM((core, 2 * band), jnp.bfloat16),
-            pltpu.VMEM((2 * MARGIN, 2 * band), jnp.bfloat16),
+            pltpu.VMEM((2, MARGIN, 2 * band), jnp.bfloat16),
             pltpu.VMEM((2, GROUP // 2 * count, 4 * band), jnp.bfloat16),
             pltpu.VMEM((conds, count, count), jnp.float32),
             pltpu.VMEM((conds, count, count), jnp.float32),

time: 64.7 us -> 58.4 us (0.903)
  Pallas kernels: 63.8 us -> 57.6 us
    pallas_call x1, Pallas kernels: 62.4 us -> 56.2 us  [on_device(): pl.pallas_call(functools.partial(kernel, tiles), out_shape=(out, out), in...]
where the time goes in v3:
time: 58.4 us; the launch traced here: 58.3 us
  Pallas kernels  57.6 us (99%)
  between operations  0.64 us (1%)
    pallas_call x1, Pallas kernels, on_device(): pl.pallas_call(functools.partial(kernel, tiles), out_shape=(out, out), in...  56.2 us

profile of v3, /device:TPU:65, one launch (start us, length us, event | category | flops | bytes accessed | tf_op | source)
XLA Modules:
  0.0 58.3 jit_solution(18317893807485095898)
XLA Ops:
  0.6 0.7 %seam.1.strip_hbm = bf16[128,128]{1,0:T(8,128)(2,1)} custom-call(bf16[1,256,256]{2,1,0:T(8,128)(2,1)} %mask_hbm.3), custom_call_target="tpu_custom_call" | custom-call | tf_op jit(solution)/shard_map/seam/pallas_call | solution.py:452
  1.4 56.2 %expose.1 = (f32[1,128,256]{2,1,0:T(8,128)S(1)}, f32[1,128,256]{2,1,0:T(8,128)S(1)}) custom-call(f32[4,24]{1,0:T(4,128)} %weight_hbm.1, f32[4]{0:T(128)} %dose_hbm.1, f32[4]{0:T(128)} %threshold_hbm.1, bf16[1,256,256]{2,1,0:T(8,128)(2,1)} %mask_hbm.3, bf16[4,24,64,128]{3,2,1,0:T(8,128)(2,1)} %kernels_hbm.1, bf16[128,128]{1,0:T(8,128)(2,1)} %seam.1.strip_hbm, ...), custom_call_target="tpu_custom_call" | custom-call | tf_op jit(solution)/shard_map/expose/pallas_call | solution.py:469
  57.5 0.7 %store.1 = (f32[1,128,256]{2,1,0:T(8,128)}, f32[1,128,256]{2,1,0:T(8,128)}) custom-call(f32[1,128,256]{2,1,0:T(8,128)S(1)} %get-tuple-element.4.high_ref, f32[1,128,256]{2,1,0:T(8,128)S(1)} %get-tuple-element.5.low_ref), custom_call_target="tpu_custom_call" | custom-call | tf_op jit(solution)/shard_map/store/pallas_call | solution.py:498

commit v4 on v3

--- a/solution.py
+++ b/solution.py
@@ -160,7 +160,7 @@
     weight_hbm,
     dose_hbm,
     threshold_hbm,
-    mask_hbm,
+    mask_ref,
     kernels_hbm,
     strip_hbm,
     columns_hbm,
@@ -176,7 +176,6 @@
     weight_ref,
     dose_ref,
     threshold_ref,
-    mask_v,
     kernels_v,
     columns_v,
     strips_v,
@@ -202,6 +201,7 @@
     level_recv,
 ):
     conds, kerns, band = kernels_v.shape[:3]
+    mask_v = mask_ref.at[0]
     core = mask_v.shape[0]
     half = core // 2
     count = own_level.shape[1]
@@ -224,7 +224,6 @@
     sibling = {"cond": 1 - cond}
 
     sources = (
-        mask_hbm.at[0],
         columns_hbm,
         strips_hbm,
         own_rows_hbm,
@@ -239,7 +238,6 @@
         *[kernels_hbm.at[c] for c in range(conds)],
     )
     targets = (
-        mask_v,
         columns_v,
         strips_v,
         own_rows_v,
@@ -256,7 +254,6 @@
     loads = [
         pltpu.make_async_copy(s, t, load_sem.at[i]) for i, (s, t) in enumerate(zip(sources, targets))
     ]
-    loads[0].start()
     barrier = pltpu.get_barrier_semaphore()
     peers = 1
     for flag, peer in ((has_far, far), (greet_left, left), (greet_right, right)):
@@ -267,8 +264,6 @@
             pl.semaphore_signal(barrier, inc=1, device_id=peer, device_id_type=MESH)
 
     pl.semaphore_signal(barrier, inc=1, device_id=sibling, device_id_type=MESH)
-    for load in loads[1:]:
-        load.start()
     from_seam = [
         (seam_left, pltpu.make_async_copy(strip_hbm, left_v, strip_sem)),
         (seam_right, pltpu.make_async_copy(strip_hbm, right_v, strip_sem)),
@@ -293,14 +288,15 @@
     to_sibling = remote(far_v.at[cond], far_v.at[cond], 3, sibling)
     from_sibling = remote(far_v.at[1 - cond], far_v.at[1 - cond], 3, sibling)
 
-    loads[0].wait()
     packed_v[0] = last_columns(mask_v)
     packed_v[1] = first_columns(mask_v)
     pl.semaphore_wait(barrier, peers)
     pl.when(greet_right)(to_right.start)
     pl.when(greet_left)(to_left.start)
-
-    for load in loads[1:]:
+    for load in loads:
+        load.start()
+
+    for load in loads:
         load.wait()
     part = dot(mask_v[...], columns_v[...])
     zero = jnp.zeros((half, LANES), jnp.bfloat16)
@@ -368,53 +364,60 @@
     rows_out = rows_out_v[cond]
     bounds = []
 
-    def blur(level):
-        fine, rest = halves(level)
-        tall = nt_dot(rows_out, jnp.concatenate([fine, rest], axis=1))
-        fine, rest = halves(tall)
-        logit = dot(jnp.concatenate([fine, rest], axis=1), cols_out_v[...])
-        if bounds:
-            bounds[0] = jnp.maximum(bounds[0], logit)
-            bounds[1] = jnp.minimum(bounds[1], logit)
-        else:
-            bounds.extend([logit, logit])
+    def blur(levels):
+        talls = []
+        for level in levels:
+            fine, rest = halves(level[...])
+            tall = nt_dot(rows_out, jnp.concatenate([fine, rest], axis=1))
+            talls.append(jnp.concatenate(halves(tall), axis=1))
+        logits = dot(jnp.concatenate(talls, axis=0), cols_out_v[...])
+        for i in range(len(levels)):
+            logit = logits[i * half : (i + 1) * half]
+            if bounds:
+                bounds[0] = jnp.maximum(bounds[0], logit)
+                bounds[1] = jnp.minimum(bounds[1], logit)
+            else:
+                bounds.extend([logit, logit])
+
+    def finish(c, level):
+        total = weight_ref[c, 0]
+        for k in range(1, kerns):
+            total += weight_ref[c, k]
+        scale = jnp.full((1, count), steepness * dose_ref[c]) / jnp.full((1, count), total)
+        own_level[c] = level * scale - steepness * threshold_ref[c]
+        copy = pltpu.make_async_remote_copy(
+            src_ref=own_level.at[c],
+            dst_ref=sib_level.at[c],
+            send_sem=level_send.at[c],
+            recv_sem=level_recv.at[c],
+            device_id=sibling,
+            device_id_type=MESH,
+        )
+        copy.start()
+        level_copies.append(copy)
 
     level_copies = []
-    ready = []
+    level = None
+    levels = []
     first_half(0)
-    level = None
     for s in range(conds * steps):
         c = s // steps
         if s + 1 < conds * steps:
             first_half(s + 1)
         level = second_half(s, level)
         if s % steps == steps - 1:
-            for ref in ready:
-                blur(ref[...])
-            ready = [own_level.at[c]]
-            total = weight_ref[c, 0]
-            for k in range(1, kerns):
-                total += weight_ref[c, k]
-            scale = jnp.full((1, count), steepness * dose_ref[c]) / jnp.full((1, count), total)
-            own_level[c] = level * scale - steepness * threshold_ref[c]
-            copy = pltpu.make_async_remote_copy(
-                src_ref=own_level.at[c],
-                dst_ref=sib_level.at[c],
-                send_sem=level_send.at[c],
-                recv_sem=level_recv.at[c],
-                device_id=sibling,
-                device_id_type=MESH,
-            )
-            copy.start()
-            level_copies.append(copy)
+            levels.append(level)
             level = None
-            if c > 0:
-                level_copies[c - 1].wait_recv()
-                ready.append(sib_level.at[c - 1])
-    for ref in ready:
-        blur(ref[...])
+            if c == conds - 2:
+                for i in range(conds - 1):
+                    finish(i, levels[i])
+    finish(conds - 1, levels[-1])
+    blur([own_level.at[c] for c in range(conds)])
+    for copy in level_copies[:-1]:
+        copy.wait_recv()
+    blur([sib_level.at[c] for c in range(conds - 1)])
     level_copies[-1].wait_recv()
-    blur(sib_level[conds - 1])
+    blur([sib_level.at[conds - 1]])
     high_ref[0] = jax.nn.sigmoid(bounds[0])
     low_ref[0] = jax.nn.sigmoid(bounds[1])
 
@@ -462,18 +465,18 @@
             pltpu.SemaphoreType.DMA,
         ],
         compiler_params=pltpu.CompilerParams(collective_id=1, has_side_effects=True),
+        cost_estimate=pl.CostEstimate(flops=10**9, bytes_accessed=4 * mask.size, transcendentals=0),
         name="seam",
     )(mask)
-    loads = 4 + len(tables) + conds
+    loads = 3 + len(tables) + conds
     out = pltpu.VMEM((1, core // 2, core), jnp.float32)
     results = pl.pallas_call(
         functools.partial(kernel, tiles),
         out_shape=(out, out),
-        in_specs=[anywhere] * (6 + len(tables)),
+        in_specs=[anywhere] * 3 + [vmem] + [anywhere] * (2 + len(tables)),
         out_specs=(vmem, vmem),
         scratch_shapes=[
             *[pltpu.SMEM(a.shape, a.dtype) for a in (socs_weight, dose, threshold)],
-            pltpu.VMEM(mask.shape[1:], mask.dtype),
             pltpu.VMEM(kernels.shape, kernels.dtype),
             *[pltpu.VMEM(t.shape, t.dtype) for t in tables],
             pltpu.VMEM((2, *strip), mask.dtype),
@@ -493,7 +496,7 @@
         ],
         compiler_params=pltpu.CompilerParams(collective_id=0, has_side_effects=True),
         name="expose",
-    )(socs_weight, dose, threshold, mask, kernels, seam, *tables)
+    )(socs_weight, dose, threshold, pltpu.with_memory_space_constraint(mask, pltpu.VMEM), kernels, seam, *tables)
     final = jax.ShapeDtypeStruct((1, core // 2, core), jnp.float32)
     return pl.pallas_call(
         store_kernel,

time: 58.4 us -> 57.5 us (0.985)
  Pallas kernels: 57.6 us -> 56.7 us
    pallas_call x1, Pallas kernels: 56.2 us -> 55.1 us  [on_device(): pl.pallas_call(functools.partial(kernel, tiles), out_shape=(out, out), in...]
where the time goes in v4:
time: 57.5 us; the launch traced here: 57.4 us
  Pallas kernels  56.7 us (99%)
  between operations  0.65 us (1%)
    pallas_call x1, Pallas kernels, on_device(): pl.pallas_call(functools.partial(kernel, tiles), out_shape=(out, out), in...  55.1 us

profile of v4, /device:TPU:65, one launch (start us, length us, event | category | flops | bytes accessed | tf_op | source)
XLA Modules:
  0.0 57.4 jit_solution(10716476252729052629)
XLA Ops:
  0.6 0.0 copy-start
  0.6 0.9 %seam.1.strip_hbm = bf16[128,128]{1,0:T(8,128)(2,1)} custom-call(bf16[1,256,256]{2,1,0:T(8,128)(2,1)} %mask_ref.1), custom_call_target="tpu_custom_call" | custom-call | flops 1000000000 | bytes 262144 | tf_op jit(solution)/shard_map/seam/pallas_call | solution.py:455
  1.5 0.0 copy-done
  1.5 55.1 %expose.1 = (f32[1,128,256]{2,1,0:T(8,128)S(1)}, f32[1,128,256]{2,1,0:T(8,128)S(1)}) custom-call(f32[4,24]{1,0:T(4,128)} %weight_hbm.1, f32[4]{0:T(128)} %dose_hbm.1, f32[4]{0:T(128)} %threshold_hbm.1, bf16[1,256,256]{2,1,0:T(8,128)(2,1)S(1)} %copy-done, bf16[4,24,64,128]{3,2,1,0:T(8,128)(2,1)} %kernels_hbm.1, bf16[128,128]{1,0:T(8,128)(2,1)} %seam.1.strip_hbm, ...), custom_call_target="tpu_custom_call" | custom-call | tf_op jit(solution)/shard_map/expose/pallas_call | solution.py:473
  56.6 0.7 %store.1 = (f32[1,128,256]{2,1,0:T(8,128)}, f32[1,128,256]{2,1,0:T(8,128)}) custom-call(f32[1,128,256]{2,1,0:T(8,128)S(1)} %get-tuple-element.4.high_ref, f32[1,128,256]{2,1,0:T(8,128)S(1)} %get-tuple-element.5.low_ref), custom_call_target="tpu_custom_call" | custom-call | tf_op jit(solution)/shard_map/store/pallas_call | solution.py:501
Async XLA Ops:
  0.6 0.9 %copy-start = (bf16[1,256,256]{2,1,0:T(8,128)(2,1)S(1)}, bf16[1,256,256]{2,1,0:T(8,128)(2,1)}, u32[]{:S(2)}) copy-start(bf16[1,256,256]{2,1,0:T(8,128)(2,1)} %mask_ref.1) | copy-start | bytes 393220

commit v5 on v4

--- a/solution.py
+++ b/solution.py
@@ -296,6 +296,16 @@
     for load in loads:
         load.start()
 
+    takes_first = jnp.logical_and(lax.rem(row, 2) == 0, column >= grid_cols // 2)
+    hand_on_early = jnp.logical_and(has_far, takes_first)
+    hand_on_late = jnp.logical_and(has_far, jnp.logical_not(takes_first))
+
+    def hand_on():
+        to_far.wait_recv()
+        to_sibling.start()
+
+    pl.when(hand_on_early)(hand_on)
+
     for load in loads:
         load.wait()
     part = dot(mask_v[...], columns_v[...])
@@ -311,11 +321,7 @@
     pl.when(has_far)(to_far.start)
     mixed = dot(own_rows_v[...], spec_rows[...])
 
-    @pl.when(has_far)
-    def _():
-        to_far.wait_recv()
-        to_sibling.start()
-
+    pl.when(hand_on_late)(hand_on)
     pl.when(has_other)(from_sibling.wait_recv)
     zero = jnp.zeros((MARGIN, 2 * band), jnp.bfloat16)
     above = jnp.where(has_up, far_v[0], zero)

time: 57.5 us -> 57 us (level)
  no operation moved by 1% of the time
where the time goes in v5:
time: 57 us; the launch traced here: 56.8 us
  Pallas kernels  56.2 us (99%)
  between operations  0.65 us (1%)
    pallas_call x1, Pallas kernels, on_device(): pl.pallas_call(functools.partial(kernel, tiles), out_shape=(out, out), in...  54.6 us

profile of v5, /device:TPU:65, one launch (start us, length us, event | category | flops | bytes accessed | tf_op | source)
XLA Modules:
  0.0 56.8 jit_solution(13855289987634534174)
XLA Ops:
  0.6 0.0 copy-start
  0.6 0.9 %seam.1.strip_hbm = bf16[128,128]{1,0:T(8,128)(2,1)} custom-call(bf16[1,256,256]{2,1,0:T(8,128)(2,1)} %mask_ref.1), custom_call_target="tpu_custom_call" | custom-call | flops 1000000000 | bytes 262144 | tf_op jit(solution)/shard_map/seam/pallas_call | solution.py:461
  1.5 0.0 copy-done
  1.5 54.6 %expose.1 = (f32[1,128,256]{2,1,0:T(8,128)S(1)}, f32[1,128,256]{2,1,0:T(8,128)S(1)}) custom-call(f32[4,24]{1,0:T(4,128)} %weight_hbm.1, f32[4]{0:T(128)} %dose_hbm.1, f32[4]{0:T(128)} %threshold_hbm.1, bf16[1,256,256]{2,1,0:T(8,128)(2,1)S(1)} %copy-done, bf16[4,24,64,128]{3,2,1,0:T(8,128)(2,1)} %kernels_hbm.1, bf16[128,128]{1,0:T(8,128)(2,1)} %seam.1.strip_hbm, ...), custom_call_target="tpu_custom_call" | custom-call | tf_op jit(solution)/shard_map/expose/pallas_call | solution.py:479
  56.1 0.7 %store.1 = (f32[1,128,256]{2,1,0:T(8,128)}, f32[1,128,256]{2,1,0:T(8,128)}) custom-call(f32[1,128,256]{2,1,0:T(8,128)S(1)} %get-tuple-element.4.high_ref, f32[1,128,256]{2,1,0:T(8,128)S(1)} %get-tuple-element.5.low_ref), custom_call_target="tpu_custom_call" | custom-call | tf_op jit(solution)/shard_map/store/pallas_call | solution.py:507
Async XLA Ops:
  0.6 0.9 %copy-start = (bf16[1,256,256]{2,1,0:T(8,128)(2,1)S(1)}, bf16[1,256,256]{2,1,0:T(8,128)(2,1)}, u32[]{:S(2)}) copy-start(bf16[1,256,256]{2,1,0:T(8,128)(2,1)} %mask_ref.1) | copy-start | bytes 393220

commit v6 on v5

--- a/solution.py
+++ b/solution.py
@@ -214,8 +214,9 @@
     has_down = row < tiles // grid_cols - 1
     greet_left = jnp.logical_and(has_left, jnp.logical_not(seam_left))
     greet_right = jnp.logical_and(has_right, jnp.logical_not(seam_right))
-    right = {"tile": lax.rem(tile + 1, tiles)}
-    left = {"tile": lax.rem(tile + tiles - 1, tiles)}
+    right_tile = lax.rem(tile + 1, tiles)
+    left_tile = lax.rem(tile + tiles - 1, tiles)
+    strips_out = cond == 1
     far = {"tile": lax.rem(tile + tiles + grid_cols * (2 * cond - 1), tiles), "cond": 1 - cond}
     far_row = row + 2 * cond - 1
     has_far = jnp.logical_and(far_row >= 0, far_row < tiles // grid_cols)
@@ -255,14 +256,18 @@
         pltpu.make_async_copy(s, t, load_sem.at[i]) for i, (s, t) in enumerate(zip(sources, targets))
     ]
     barrier = pltpu.get_barrier_semaphore()
-    peers = 1
-    for flag, peer in ((has_far, far), (greet_left, left), (greet_right, right)):
-        peers = peers + flag.astype(jnp.int32)
+    for flag, peer in (
+        (greet_left, {"tile": left_tile, "cond": 1}),
+        (greet_right, {"tile": right_tile, "cond": 1}),
+        (has_far, far),
+    ):
 
         @pl.when(flag)
         def _(peer=peer):
             pl.semaphore_signal(barrier, inc=1, device_id=peer, device_id_type=MESH)
 
+    beside = greet_left.astype(jnp.int32) + greet_right.astype(jnp.int32)
+    peers = 1 + has_far.astype(jnp.int32) + 2 * cond * beside
     pl.semaphore_signal(barrier, inc=1, device_id=sibling, device_id_type=MESH)
     from_seam = [
         (seam_left, pltpu.make_async_copy(strip_hbm, left_v, strip_sem)),
@@ -281,22 +286,44 @@
             device_id_type=MESH,
         )
 
-    to_right = remote(packed_v.at[0], left_v, 0, right)
-    to_left = remote(packed_v.at[1], right_v, 1, left)
+    to_right, to_left = [
+        [
+            pltpu.make_async_remote_copy(
+                src_ref=packed_v.at[side],
+                dst_ref=strip_v,
+                send_sem=send_sem.at[4 + 2 * side + i],
+                recv_sem=recv_sem.at[side],
+                device_id={"tile": peer, "cond": i},
+                device_id_type=MESH,
+            )
+            for i in range(2)
+        ]
+        for side, strip_v, peer in ((0, left_v, right_tile), (1, right_v, left_tile))
+    ]
+    from_left, from_right = to_right[0], to_left[0]
+    send_right = jnp.logical_and(greet_right, strips_out)
+    send_left = jnp.logical_and(greet_left, strips_out)
     edge = pl.ds(pl.multiple_of(cond * (core - MARGIN), MARGIN), MARGIN)
     to_far = remote(spec_rows.at[edge], far_v.at[1 - cond], 2, far)
     to_sibling = remote(far_v.at[cond], far_v.at[cond], 3, sibling)
     from_sibling = remote(far_v.at[1 - cond], far_v.at[1 - cond], 3, sibling)
 
+    takes_first = jnp.logical_and(lax.rem(row, 2) == 0, column >= grid_cols // 2)
+
+    def start_loads():
+        for load in loads:
+            load.start()
+
+    pl.when(takes_first)(start_loads)
     packed_v[0] = last_columns(mask_v)
+    pl.semaphore_wait(barrier, peers)
+    for copy in to_right:
+        pl.when(send_right)(copy.start)
     packed_v[1] = first_columns(mask_v)
-    pl.semaphore_wait(barrier, peers)
-    pl.when(greet_right)(to_right.start)
-    pl.when(greet_left)(to_left.start)
-    for load in loads:
-        load.start()
-
-    takes_first = jnp.logical_and(lax.rem(row, 2) == 0, column >= grid_cols // 2)
+    for copy in to_left:
+        pl.when(send_left)(copy.start)
+    pl.when(jnp.logical_not(takes_first))(start_loads)
+
     hand_on_early = jnp.logical_and(has_far, takes_first)
     hand_on_late = jnp.logical_and(has_far, jnp.logical_not(takes_first))
 
@@ -312,8 +339,8 @@
     zero = jnp.zeros((half, LANES), jnp.bfloat16)
     pl.when(seam_left)(from_seam[0][1].wait)
     pl.when(seam_right)(from_seam[1][1].wait)
-    pl.when(greet_left)(to_right.wait_recv)
-    pl.when(greet_right)(to_left.wait_recv)
+    pl.when(greet_left)(from_left.wait_recv)
+    pl.when(greet_right)(from_right.wait_recv)
     aside = dot(jnp.where(has_left, left_v[...], zero), strips_v[0])
     aside += dot(jnp.where(has_right, right_v[...], zero), strips_v[1])
     spec_rows[:half] = (part[:half] + aside[:, : 2 * band]).astype(jnp.bfloat16)
@@ -428,8 +455,10 @@
     low_ref[0] = jax.nn.sigmoid(bounds[1])
 
     for flag, copy in (
-        (greet_right, to_right),
-        (greet_left, to_left),
+        (send_right, to_right[0]),
+        (send_right, to_right[1]),
+        (send_left, to_left[0]),
+        (send_left, to_left[1]),
         (has_far, to_far),
         (has_far, to_sibling),
     ):
@@ -495,7 +524,7 @@
             pltpu.VMEM((conds, count, count), jnp.float32),
             pltpu.SemaphoreType.DMA((loads,)),
             pltpu.SemaphoreType.DMA,
-            pltpu.SemaphoreType.DMA((4,)),
+            pltpu.SemaphoreType.DMA((8,)),
             pltpu.SemaphoreType.DMA((4,)),
             pltpu.SemaphoreType.DMA((conds,)),
             pltpu.SemaphoreType.DMA((conds,)),

time: 57 us -> 56.7 us (level)
  no operation moved by 1% of the time
where the time goes in v6:
time: 56.7 us; the launch traced here: 56.5 us
  Pallas kernels  55.9 us (99%)
  between operations  0.65 us (1%)
    pallas_call x1, Pallas kernels, on_device(): pl.pallas_call(functools.partial(kernel, tiles), out_shape=(out, out), in...  54.3 us

profile of v6, /device:TPU:65, one launch (start us, length us, event | category | flops | bytes accessed | tf_op | source)
XLA Modules:
  0.0 56.5 jit_solution(9717452869917028357)
XLA Ops:
  0.6 0.0 copy-start
  0.6 0.9 %seam.1.strip_hbm = bf16[128,128]{1,0:T(8,128)(2,1)} custom-call(bf16[1,256,256]{2,1,0:T(8,128)(2,1)} %mask_ref.1), custom_call_target="tpu_custom_call" | custom-call | flops 1000000000 | bytes 262144 | tf_op jit(solution)/shard_map/seam/pallas_call | solution.py:490
  1.5 0.0 copy-done
  1.5 54.3 %expose.1 = (f32[1,128,256]{2,1,0:T(8,128)S(1)}, f32[1,128,256]{2,1,0:T(8,128)S(1)}) custom-call(f32[4,24]{1,0:T(4,128)} %weight_hbm.1, f32[4]{0:T(128)} %dose_hbm.1, f32[4]{0:T(128)} %threshold_hbm.1, bf16[1,256,256]{2,1,0:T(8,128)(2,1)S(1)} %copy-done, bf16[4,24,64,128]{3,2,1,0:T(8,128)(2,1)} %kernels_hbm.1, bf16[128,128]{1,0:T(8,128)(2,1)} %seam.1.strip_hbm, ...), custom_call_target="tpu_custom_call" | custom-call | tf_op jit(solution)/shard_map/expose/pallas_call | solution.py:508
  55.8 0.7 %store.1 = (f32[1,128,256]{2,1,0:T(8,128)}, f32[1,128,256]{2,1,0:T(8,128)}) custom-call(f32[1,128,256]{2,1,0:T(8,128)S(1)} %get-tuple-element.4.high_ref, f32[1,128,256]{2,1,0:T(8,128)S(1)} %get-tuple-element.5.low_ref), custom_call_target="tpu_custom_call" | custom-call | tf_op jit(solution)/shard_map/store/pallas_call | solution.py:536
Async XLA Ops:
  0.6 0.9 %copy-start = (bf16[1,256,256]{2,1,0:T(8,128)(2,1)S(1)}, bf16[1,256,256]{2,1,0:T(8,128)(2,1)}, u32[]{:S(2)}) copy-start(bf16[1,256,256]{2,1,0:T(8,128)(2,1)} %mask_ref.1) | copy-start | bytes 393220

commit v7 on v6

--- a/solution.py
+++ b/solution.py
@@ -256,6 +256,7 @@
         pltpu.make_async_copy(s, t, load_sem.at[i]) for i, (s, t) in enumerate(zip(sources, targets))
     ]
     barrier = pltpu.get_barrier_semaphore()
+    pl.semaphore_signal(barrier, inc=1, device_id=sibling, device_id_type=MESH)
     for flag, peer in (
         (greet_left, {"tile": left_tile, "cond": 1}),
         (greet_right, {"tile": right_tile, "cond": 1}),
@@ -268,7 +269,6 @@
 
     beside = greet_left.astype(jnp.int32) + greet_right.astype(jnp.int32)
     peers = 1 + has_far.astype(jnp.int32) + 2 * cond * beside
-    pl.semaphore_signal(barrier, inc=1, device_id=sibling, device_id_type=MESH)
     from_seam = [
         (seam_left, pltpu.make_async_copy(strip_hbm, left_v, strip_sem)),
         (seam_right, pltpu.make_async_copy(strip_hbm, right_v, strip_sem)),
@@ -437,13 +437,13 @@
         c = s // steps
         if s + 1 < conds * steps:
             first_half(s + 1)
+        if s == (conds - 1) * steps:
+            for i in range(conds - 1):
+                finish(i, levels[i])
         level = second_half(s, level)
         if s % steps == steps - 1:
             levels.append(level)
             level = None
-            if c == conds - 2:
-                for i in range(conds - 1):
-                    finish(i, levels[i])
     finish(conds - 1, levels[-1])
     blur([own_level.at[c] for c in range(conds)])
     for copy in level_copies[:-1]:

time: 56.7 us -> 56.6 us (level)
  no operation moved by 1% of the time
where the time goes in v7:
time: 56.6 us; the launch traced here: 56.4 us
  Pallas kernels  55.8 us (99%)
  between operations  0.65 us (1%)
    pallas_call x1, Pallas kernels, on_device(): pl.pallas_call(functools.partial(kernel, tiles), out_shape=(out, out), in...  54.2 us

profile of v7, /device:TPU:65, one launch (start us, length us, event | category | flops | bytes accessed | tf_op | source)
XLA Modules:
  0.0 56.4 jit_solution(4720913235546450039)
XLA Ops:
  0.6 0.0 copy-start
  0.6 0.9 %seam.1.strip_hbm = bf16[128,128]{1,0:T(8,128)(2,1)} custom-call(bf16[1,256,256]{2,1,0:T(8,128)(2,1)} %mask_ref.1), custom_call_target="tpu_custom_call" | custom-call | flops 1000000000 | bytes 262144 | tf_op jit(solution)/shard_map/seam/pallas_call | solution.py:490
  1.5 0.0 copy-done
  1.5 54.2 %expose.1 = (f32[1,128,256]{2,1,0:T(8,128)S(1)}, f32[1,128,256]{2,1,0:T(8,128)S(1)}) custom-call(f32[4,24]{1,0:T(4,128)} %weight_hbm.1, f32[4]{0:T(128)} %dose_hbm.1, f32[4]{0:T(128)} %threshold_hbm.1, bf16[1,256,256]{2,1,0:T(8,128)(2,1)S(1)} %copy-done, bf16[4,24,64,128]{3,2,1,0:T(8,128)(2,1)} %kernels_hbm.1, bf16[128,128]{1,0:T(8,128)(2,1)} %seam.1.strip_hbm, ...), custom_call_target="tpu_custom_call" | custom-call | tf_op jit(solution)/shard_map/expose/pallas_call | solution.py:508
  55.7 0.7 %store.1 = (f32[1,128,256]{2,1,0:T(8,128)}, f32[1,128,256]{2,1,0:T(8,128)}) custom-call(f32[1,128,256]{2,1,0:T(8,128)S(1)} %get-tuple-element.4.high_ref, f32[1,128,256]{2,1,0:T(8,128)S(1)} %get-tuple-element.5.low_ref), custom_call_target="tpu_custom_call" | custom-call | tf_op jit(solution)/shard_map/store/pallas_call | solution.py:536
Async XLA Ops:
  0.6 0.9 %copy-start = (bf16[1,256,256]{2,1,0:T(8,128)(2,1)S(1)}, bf16[1,256,256]{2,1,0:T(8,128)(2,1)}, u32[]{:S(2)}) copy-start(bf16[1,256,256]{2,1,0:T(8,128)(2,1)} %mask_ref.1) | copy-start | bytes 393220
